TPU v7x, 32 devices: a whole 2x2x4 slice. The times are simulated.
32 devices in a mesh: depth: 2 (over core), tile: 16 (over z, y, x).
Axes of the slice: x: 2, y: 2, z: 4, core: 2. Of those that a mesh axis runs over, the one named last changes fastest.
Arguments:
- volume: float32 [8, 512, 1024], P('depth', 'tile'), may hold values from -6 to 6
- measured: float32 [3, 512, 1024], P(None, 'tile'), may hold values from -12 to 12
- row_bank: float32 [256, 2, 33], replicated, may hold values from -1 to 1
- col_bank: float32 [256, 2, 33], replicated, may hold values from -1 to 1
- kernel_index: int32 [169, 8], P(None, 'depth'), may hold values from 0 to 255
- view_order: int32 [3], replicated, may hold values from 0 to 168
Outputs:
- volume_out: float32 [8, 512, 1024], P('depth', 'tile')
- last_residual: float32 [512, 1024], P('tile')
All inputs are finite; a program needn't handle non-finite values.
Results may differ from a plain program's by a relative error of at most 0.00013.
Values sent between devices are 32-bit elements; how exact they have to be, the bound alone decides.
No kernel may reach another device: no remote copies, remote signals or barrier semaphores. Data moves between devices by JAX's collectives and lax.ppermute only.
A program may use at most 64 MiB of HBM per device.

v0:
```python
import functools

import jax
import jax.numpy as jnp
from jax import lax
from jax.experimental import pallas as pl
from jax.experimental.pallas import tpu as pltpu
from jax.sharding import PartitionSpec as P

descent_step = 0.5
shrinkage = 0.1
LANES = 128
HALF = LANES // 2
bf16, f32 = jnp.bfloat16, jnp.float32


def split(x):
    hi = x.astype(bf16)
    return hi, (x - hi.astype(f32)).astype(bf16)


def dot(a, b):
    return lax.dot_general(a, b, (((1,), (0,)), ((), ())), preferred_element_type=f32)


def dot_nt(a, b):
    return lax.dot_general(a, b, (((1,), (1,)), ((), ())), preferred_element_type=f32)


def lane_iota(shape):
    return lax.broadcasted_iota(jnp.int32, shape, 1)


def row_iota(shape):
    return lax.broadcasted_iota(jnp.int32, shape, 0)


class Place:
    def __init__(self, paired):
        d, t = lax.axis_index("depth"), lax.axis_index("tile")
        tiles = lax.axis_size("tile")
        odd = lax.rem(t, 2)
        self.first = t == 0
        self.last = t == tiles - 1
        self.flag = 1 - jnp.bitwise_xor(odd, d) if paired else 1 - odd
        end = jnp.logical_and(jnp.logical_or(self.first, self.last), paired)
        self.end_even = jnp.logical_and(end, d == 0)
        self.end_odd = jnp.logical_and(end, d == 1)


def pick_taps(steps, planes, view_ref, index, banks, taps_ref):
    count = taps_ref.shape[1]
    index = index.astype(f32)
    copies = jnp.concatenate([index] * (count // planes), axis=0)
    line, lane = row_iota(copies.shape), lane_iota(copies.shape)
    view = jnp.full(copies.shape, view_ref[0], jnp.int32)
    for step in range(1, steps):
        view = jnp.where(line >= step * planes, view_ref[step], view)
    entry = jnp.sum(jnp.where(lane == view, copies, 0.0), axis=1, keepdims=True)
    size = banks[0].shape[2]
    chosen = (lane_iota((count, size)).astype(f32) == entry).astype(f32).astype(bf16)
    taps_ref[...] = jnp.zeros(taps_ref.shape, f32)
    for b, bank in enumerate(banks):
        for r in range(2):
            hi, lo = split(bank[:, r, :])
            taps = dot_nt(chosen, hi) + dot_nt(chosen, lo)
            taps_ref[2 * b + r, :, 0 : taps.shape[1]] = taps


def column_operands(taps_ref, line, d, reach, forward_out, adjoint_out):
    square = (LANES, LANES)
    below = lane_iota(square) < row_iota(square)
    above = lane_iota(square) > row_iota(square)
    for r in range(2):
        base = pltpu.roll(
            jnp.broadcast_to(taps_ref[2 + r, line : line + 1], (8, LANES)),
            (LANES - HALF - reach) % LANES, 1, stride=1, stride_axis=0,
        )
        ring = jnp.concatenate(
            [base] + [pltpu.roll(base, 8 * b, 1) for b in range(1, LANES // 8)], axis=0
        )
        low_hi, low_lo = split(jnp.where(below, ring, 0.0))
        up_hi, up_lo = split(jnp.where(above, ring, 0.0))
        left, right = slice(0, LANES), slice(LANES, 2 * LANES)
        if forward_out is not None:
            fwd_hi, fwd_lo = forward_out
            here = slice(r * LANES, (r + 1) * LANES)
            fwd_hi[d, here, left] = up_hi
            fwd_hi[d, here, right] = low_hi
            fwd_lo[d, here, left] = up_lo
            fwd_lo[d, here, right] = low_lo
        if adjoint_out is not None:
            adjoint_out[d, r, left, left] = low_hi
            adjoint_out[d, r, left, right] = low_lo
            adjoint_out[d, r, right, left] = up_hi
            adjoint_out[d, r, right, right] = up_lo


def row_operand(taps_ref, step, planes, reach, place):
    rows = 2 * reach
    per_lane = LANES // rows
    window, lane = row_iota((8, LANES)), lane_iota((8, LANES)) // rows
    parts = []
    for k in range(2 * planes):
        line = step * planes + k // 2
        parts.append(
            pltpu.roll(
                jnp.broadcast_to(taps_ref[k % 2, line : line + 1], (8, LANES)),
                ((k % per_lane) * rows - 2 * reach) % LANES, 1, stride=1, stride_axis=0,
            )
        )
    bands = []
    for band in range(2 * rows // 8):
        start = (8 * band) % rows
        offset = start + rows * (place.flag if band < rows // 8 else 1 - place.flag)
        spot = window + offset
        good = jnp.logical_and(
            jnp.logical_or(jnp.logical_not(place.first), spot >= reach),
            jnp.logical_or(jnp.logical_not(place.last), spot < rows + reach),
        )
        line = []
        for group in range(2 * planes // per_lane):
            total = jnp.zeros((8, LANES), f32)
            for k in range(per_lane):
                part = pltpu.roll(parts[group * per_lane + k], offset, 1)
                total = jnp.where(lane == k, part, total)
            line.append(jnp.where(good, total, 0.0))
        bands.append(jnp.concatenate(line, axis=1))
    return jnp.concatenate(bands, axis=0)


def adjoint_row_operand(stack):
    hi, lo = split(stack.T)
    return jnp.concatenate([hi, hi, lo], axis=1)


def forward(volume, fwd_hi, fwd_lo, row_hi, row_lo, target, w_hi, w_lo):
    planes = len(volume)
    rows, width = volume[0].shape
    blocks = width // LANES
    zero = jnp.zeros((rows, LANES), bf16)
    left = lane_iota((rows, LANES)) < HALF
    for d in range(planes):
        sides = []
        for part in split(volume[d]):
            column = [zero] + [part[:, b * LANES : (b + 1) * LANES] for b in range(blocks)] + [zero]
            column = jnp.concatenate(column, axis=0)
            sides.append(jnp.concatenate([column[:-rows], column[rows:]], axis=1))
        hi, lo = sides
        wide = dot_nt(hi, fwd_hi[d]) + dot_nt(lo, fwd_hi[d]) + dot_nt(hi, fwd_lo[d])
        for r in range(2):
            part = wide[:, r * LANES : (r + 1) * LANES]
            spot = pl.ds((2 * d + r) * rows, rows)
            for c in range(blocks):
                block = part[c * rows : (c + 1) * rows]
                if c == 0:
                    block = jnp.where(left, part[blocks * rows :], block)
                hi_w, lo_w = split(block)
                w_hi[spot, c * LANES : (c + 1) * LANES] = hi_w
                w_lo[spot, c * LANES : (c + 1) * LANES] = lo_w
    image = dot(row_hi, w_hi[...]) + dot(row_lo, w_hi[...]) + dot(row_hi, w_lo[...])
    return image[:rows] - target, image[rows:]


def adjoint(residual, adj_rows, adj, volume, emit):
    planes = len(volume)
    rows, width = volume[0].shape
    blocks = width // LANES
    hi, lo = split(residual)
    upper = dot(adj_rows, jnp.concatenate([hi, lo, hi], axis=0))
    left = lane_iota((rows, LANES)) < HALF
    result = []
    for d in range(planes):
        total = None
        for r in range(2):
            spot = (2 * d + r) * rows
            part = upper[spot : spot + rows]
            edge = part[:, :LANES]
            column = [jnp.where(left, 0.0, edge)]
            column += [part[:, b * LANES : (b + 1) * LANES] for b in range(1, blocks)]
            column += [jnp.where(left, edge, 0.0)]
            for side in split(jnp.concatenate(column, axis=0)):
                side = jnp.concatenate([side[:-rows], side[rows:]], axis=1)
                term = dot(side, adj[d, r])
                total = term if total is None else total + term
        grad = total[:, :LANES] + total[:, LANES:]
        grad = jnp.concatenate([grad[c * rows : (c + 1) * rows] for c in range(blocks)], axis=1)
        moved = volume[d] - descent_step * grad
        plane = moved - jnp.clip(moved, -shrinkage, shrinkage)
        emit(d, plane)
        result.append(plane)
    return result


def window_target(measured, place):
    reach = measured.shape[0] // 2
    upper = jnp.where(place.flag == 1, measured[reach:], 0.0)
    lower = jnp.where(place.flag == 1, 0.0, measured[:reach])
    return pltpu.roll(jnp.concatenate([upper, lower], axis=0), HALF, 1)


def joined(place, kept, crossed, swapped):
    add = jnp.where(place.end_even, swapped, jnp.where(place.end_odd, 0.0, crossed))
    other = jnp.where(
        place.end_even, crossed, jnp.where(place.end_odd, crossed + swapped, swapped)
    )
    return kept + add, other


def first_kernel(
    paired, view, index, row_bank, col_bank, volume, measured, mine, other, taps,
    index_v, row_v, col_v, volume_v, measured_v, fwd_hi, fwd_lo, w_hi, w_lo, sems,
):
    pairs = [
        (index, index_v), (col_bank, col_v), (row_bank, row_v), (volume, volume_v),
        (measured.at[0], measured_v),
    ]
    copies = [pltpu.make_async_copy(a, b, sems.at[i]) for i, (a, b) in enumerate(pairs)]
    for copy in copies:
        copy.start()
    place = Place(paired)
    planes = volume.shape[0]
    reach = (row_bank.shape[0] - 1) // 2
    for copy in copies[:3]:
        copy.wait()
    pick_taps(view.shape[0], planes, view, index_v[...], (row_v, col_v), taps)
    for d in range(planes):
        column_operands(taps, d, d, reach, (fwd_hi, fwd_lo), None)
    row_hi, row_lo = split(row_operand(taps, 0, planes, reach, place))
    for copy in copies[3:]:
        copy.wait()
    target = window_target(measured_v[...], place) if paired else 0.0
    mine[...], other[...] = forward(
        [volume_v[d] for d in range(planes)], fwd_hi, fwd_lo, row_hi, row_lo, target, w_hi, w_lo
    )


def prepare_kernel(paired, planes, reach, back, ahead, taps, *outs):
    place = Place(paired)
    fwd_hi, fwd_lo, row_hi, row_lo = outs[:4]
    wanted = sorted(set(back) | {ahead})
    for step in wanted:
        adj, adj_rows = outs[4 + 2 * back.index(step) :][:2] if step in back else (None, None)
        for d in range(planes):
            column_operands(
                taps, step * planes + d, d, reach, (fwd_hi, fwd_lo) if step == ahead else None, adj
            )
        stack = row_operand(taps, step, planes, reach, place)
        if step == ahead:
            row_hi[...], row_lo[...] = split(stack)
        if step in back:
            adj_rows[...] = adjoint_row_operand(stack)


def middle_kernel(
    paired, step, kept, crossed, swapped, adj, adj_rows, fwd_hi, fwd_lo, row_hi, row_lo,
    volume, measured, mine, other, fresh, w_hi, w_lo,
):
    place = Place(paired)
    residual = jnp.concatenate(joined(place, kept[...], crossed[...], swapped[...]), axis=0)

    def emit(d, plane):
        fresh[d] = plane

    planes = [volume[d] for d in range(volume.shape[0])]
    planes = adjoint(residual, adj_rows[...], adj, planes, emit)
    target = window_target(measured[step], place) if paired else 0.0
    mine[...], other[...] = forward(
        planes, fwd_hi, fwd_lo, row_hi[...], row_lo[...], target, w_hi, w_lo
    )


def last_kernel(
    paired, kept, crossed, swapped, adj, adj_rows, volume, fresh, residual_out,
    fresh_v, residual_v, sems,
):
    place = Place(paired)
    mine, other = joined(place, kept[...], crossed[...], swapped[...])
    reach = mine.shape[0] // 2
    lower = place.flag == 1
    own = jnp.concatenate(
        [jnp.where(lower, other[reach:], mine[reach:]), jnp.where(lower, mine[:reach], other[:reach])],
        axis=0,
    )
    residual_v[...] = pltpu.roll(own, own.shape[1] - HALF, 1)
    count = volume.shape[0]
    copies = [pltpu.make_async_copy(fresh_v.at[d], fresh.at[d], sems.at[d]) for d in range(count)]
    copies.append(pltpu.make_async_copy(residual_v, residual_out, sems.at[count]))
    copies[count].start()

    def emit(d, plane):
        fresh_v[d] = plane
        copies[d].start()

    planes = [volume[d] for d in range(count)]
    adjoint(jnp.concatenate([mine, other], axis=0), adj_rows[...], adj, planes, emit)
    for copy in copies:
        copy.wait()


VMEM = pl.BlockSpec(memory_space=pltpu.VMEM)
SMEM = pl.BlockSpec(memory_space=pltpu.SMEM)
HBM = pl.BlockSpec(memory_space=pltpu.HBM)


def call(kernel, in_specs, out_specs, outs, scratch, flops, name, args):
    return pl.pallas_call(
        kernel,
        out_shape=outs,
        in_specs=in_specs,
        out_specs=out_specs,
        scratch_shapes=scratch,
        compiler_params=pltpu.CompilerParams(vmem_limit_bytes=24 << 20),
        cost_estimate=pl.CostEstimate(flops=flops, bytes_accessed=4 << 20, transcendentals=0),
        name=name,
    )(*args)


def per_device(volume, measured, row_bank, col_bank, kernel_index, view_order):
    planes, rows, width = volume.shape
    steps = measured.shape[0]
    reach = (row_bank.shape[2] - 1) // 2
    assert rows == 2 * reach and width % LANES == 0 and reach <= HALF
    depth, tiles = lax.axis_size("depth"), lax.axis_size("tile")
    d, t = lax.axis_index("depth"), lax.axis_index("tile")
    paired = depth == 2 and tiles % 2 == 0 and tiles > 2
    place = Place(paired)

    def flow(spot):
        side, i = divmod(spot, tiles)
        ends = (0, tiles - 1)
        if side == 1:
            return i if i in ends else tiles + (i + 1 if i % 2 else i - 1)
        return tiles + (i ^ 1) if (i ^ 1) in ends else i ^ 1

    def exchange(mine, other, step, during):
        if paired:
            swap = [(0, 1), (1, 0)]
            kept = mine + lax.ppermute(other, "depth", swap)
            crossed = lax.ppermute(
                kept, ("depth", "tile"), [(i, flow(i)) for i in range(2 * tiles)]
            )
            ready = during()
            if ready:
                crossed, *ready = lax.optimization_barrier((crossed, *ready))
            send = jnp.where(place.end_odd, 0.0, kept) + jnp.where(place.end_even, 0.0, crossed)
            return kept, crossed, lax.ppermute(send, "depth", swap), ready
        target = jnp.roll(measured[step], HALF, axis=1)
        high = jnp.pad(target[:reach], ((reach, 0), (0, 0)))
        low = jnp.pad(target[reach:], ((0, reach), (0, 0)))
        lower = place.flag == 1
        evens = [(i, i ^ 1) for i in range(tiles) if i ^ 1 < tiles]
        odds = [(i, i + 1 if i % 2 else i - 1) for i in range(tiles)]
        odds = [(i, j) for i, j in odds if 0 <= j < tiles]
        kept = lax.psum(mine, "depth") - jnp.where(lower, low, high)
        rest = lax.psum(other, "depth") - jnp.where(lower, high, low)
        rest = rest + lax.ppermute(rest, "tile", odds)
        return kept, lax.ppermute(kept, "tile", evens), rest, during()

    shape = jax.ShapeDtypeStruct
    stacks = 2 * planes * rows
    forward_shapes = [
        shape((planes, 2 * LANES, 2 * LANES), bf16),
        shape((planes, 2 * LANES, 2 * LANES), bf16),
        shape((2 * rows, stacks), bf16),
        shape((2 * rows, stacks), bf16),
    ]
    adjoint_shapes = [
        shape((planes, 2, 2 * LANES, 2 * LANES), bf16),
        shape((stacks, 6 * rows), bf16),
    ]
    image = shape((rows, width), f32)
    block = shape(volume.shape, f32)
    lines = -(-steps * planes // 16) * 16
    tap_shape = shape((4, lines, LANES), f32)
    scratch = [pltpu.VMEM((stacks, width), bf16)] * 2
    work = 400 << 20

    index = kernel_index.T
    banks = [jnp.transpose(x, (2, 1, 0)) for x in (row_bank, col_bank)]
    mine, other, taps = call(
        functools.partial(first_kernel, paired), [SMEM] + [HBM] * 5, [VMEM] * 3,
        [image, image, tap_shape],
        [pltpu.VMEM(x.shape, x.dtype) for x in (index, *banks, volume, measured[0])]
        + [pltpu.VMEM(x.shape, x.dtype) for x in forward_shapes[:2]]
        + scratch + [pltpu.SemaphoreType.DMA((5,))],
        work, "first", (view_order, index, *banks, volume, measured),
    )

    def prepare(back, ahead):
        outs = forward_shapes + adjoint_shapes * len(back)
        return call(
            functools.partial(prepare_kernel, paired, planes, reach, back, ahead),
            [VMEM], [VMEM] * len(outs), outs, [], work, "prepare", (taps,),
        )

    adjoints = []
    for step in range(1, steps):
        back = (0, 1) if step == 1 else (step,)
        kept, crossed, swapped, ready = exchange(
            mine, other, step - 1, lambda: prepare(back, step)
        )
        forwards = ready[:4]
        adjoints += [ready[i : i + 2] for i in range(4, len(ready), 2)]
        mine, other, volume = call(
            functools.partial(middle_kernel, paired, step), [VMEM] * 11, [VMEM] * 3,
            [image, image, block], scratch, 2 * work, "middle",
            (kept, crossed, swapped, *adjoints[step - 1], *forwards, volume, measured),
        )
    kept, crossed, swapped, _ = exchange(mine, other, steps - 1, lambda: [])
    return call(
        functools.partial(last_kernel, paired), [VMEM] * 6, [HBM] * 2, [block, image],
        [pltpu.VMEM(volume.shape, f32), pltpu.VMEM((rows, width), f32),
         pltpu.SemaphoreType.DMA((planes + 1,))],
        work, "last", (kept, crossed, swapped, *adjoints[steps - 1], volume),
    )


def solution(mesh):
    return jax.shard_map(
        per_device,
        mesh=mesh,
        in_specs=(P("depth", "tile", None), P(None, "tile", None), P(), P(), P(None, "depth"), P()),
        out_specs=(P("depth", "tile", None), P("tile", None)),
        check_vma=False,
    )
```

profile of v0, /device:TPU:11, one launch (start us, length us, event | category | flops | bytes accessed | tf_op | source)
XLA Modules:
  0.0 41.6 jit_solution(8306814651093800089)
XLA Ops:
  0.6 0.0 copy-start.6
  0.6 0.0 copy-start.7
  0.7 0.7 %copy-done.6 = s32[169,4]{0,1:T(4,128)S(1)} copy-done((s32[169,4]{0,1:T(4,128)S(1)}, s32[169,4]{0,1:T(4,128)}, u32[]{:S(2)}) %copy-start.6) | copy-done | bytes 2728
  1.3 1.0 %copy-done = f32[3,32,1024]{2,1,0:T(8,128)S(1)} copy-done((f32[3,32,1024]{2,1,0:T(8,128)S(1)}, f32[3,32,1024]{2,1,0:T(8,128)}, u32[]{:S(2)}) %copy-start) | copy-done | bytes 393240
  2.3 1.0 %copy-done.2 = f32[4,32,1024]{2,1,0:T(8,128)S(1)} copy-done((f32[4,32,1024]{2,1,0:T(8,128)S(1)}, f32[4,32,1024]{2,1,0:T(8,128)}, u32[]{:S(2)}) %copy-start.2) | copy-done | bytes 524312
  3.4 0.9 %copy-done.4 = f32[256,2,33]{0,1,2:T(2,128)S(1)} copy-done((f32[256,2,33]{0,1,2:T(2,128)S(1)}, f32[256,2,33]{0,1,2:T(2,128)}, u32[]{:S(2)}) %copy-start.4) | copy-done | bytes 67608
  4.2 0.9 %copy-done.5 = f32[256,2,33]{0,1,2:T(2,128)S(1)} copy-done((f32[256,2,33]{0,1,2:T(2,128)S(1)}, f32[256,2,33]{0,1,2:T(2,128)}, u32[]{:S(2)}) %copy-start.5) | copy-done | bytes 67608
  5.1 3.0 %first.1 = (f32[32,1024]{1,0:T(8,128)S(1)}, f32[32,1024]{1,0:T(8,128)S(1)}, f32[4,16,128]{2,1,0:T(8,128)S(1)}) custom-call(s32[3]{0:T(128)S(1)} %copy-done.7, s32[4,169]{1,0:T(4,128)S(1)} %bitcast.5, f32[33,2,256]{2,1,0:T(2,128)S(1)} %bitcast.3, f32[33,2,256]{2,1,0:T(2,128)S(1)} %bitcast.4, f32[4,32,1024]{2,1,0:T(8,128)S(1)} %copy-done.2, ...), custom_call_target="tpu_custom_call" | custom-call | flops 419430400 | bytes 4194304 | tf_op jit(solution)/shard_map/first/pallas_call | solution.py:307
  8.2 0.7 %collective-permute-start = (f32[32,1024]{1,0:T(8,128)S(1)}, f32[32,1024]{1,0:T(8,128)S(1)}, u32[]{:S(2)}, u32[]{:S(2)}) collective-permute-start(f32[32,1024]{1,0:T(8,128)S(1)} %get-tuple-element.42), channel_id=1, source_target_pairs={{0,16},{16,0},{1,17},{17,1},{2,18},{18,2},{3,19},{19,3},{4,20},{20... | collective-permute-start | bytes 393224 | tf_op jit(solution)/shard_map/ppermute | solution.py:339
  8.9 1.0 %collective-permute-done = f32[32,1024]{1,0:T(8,128)S(1)} collective-permute-done((f32[32,1024]{1,0:T(8,128)S(1)}, f32[32,1024]{1,0:T(8,128)S(1)}, u32[]{:S(2)}, u32[]{:S(2)}) %collective-permute-start) | collective-permute-done | bytes 131104 | tf_op jit(solution)/shard_map/ppermute | solution.py:339
  9.9 1.3 %collective-permute-start.1 = (f32[32,1024]{1,0:T(8,128)S(1)}, f32[32,1024]{1,0:T(8,128)S(1)}, u32[]{:S(2)}, u32[]{:S(2)}) collective-permute-start(f32[32,1024]{1,0:T(8,128)S(1)} %add.18.kept), channel_id=1, source_target_pairs={{0,1},{1,16},{2,3},{3,2},{4,5},{5,4},{6,7},{7,6},{8,9},{9,8},{10,1... | collective-permute-start | bytes 393224 | tf_op jit(solution)/shard_map/ppermute | solution.py:340
  11.2 1.8 %prepare.2 = (bf16[4,256,256]{2,1,0:T(8,128)(2,1)S(1)}, bf16[4,256,256]{2,1,0:T(8,128)(2,1)S(1)}, bf16[64,256]{1,0:T(8,128)(2,1)S(1)}, bf16[64,256]{1,0:T(8,128)...) custom-call(f32[4,16,128]{2,1,0:T(8,128)S(1)} %get-tuple-element.43.taps), custom_call_target="tpu_custom_call" | custom-call | flops 419430400 | bytes 4194304 | tf_op jit(solution)/shard_map/prepare/pallas_call | solution.py:307
  13.0 0.0 copy-start.1
  13.0 2.2 %collective-permute-done.1.crossed = f32[32,1024]{1,0:T(8,128)S(1)} collective-permute-done((f32[32,1024]{1,0:T(8,128)S(1)}, f32[32,1024]{1,0:T(8,128)S(1)}, u32[]{:S(2)}, u32[]{:S(2)}) %collective-permute-start.1) | collective-permute-done | bytes 131104 | tf_op jit(solution)/shard_map/ppermute | solution.py:340
  15.2 1.6 %collective-permute-start.2 = (f32[32,1024]{1,0:T(8,128)S(1)}, f32[32,1024]{1,0:T(8,128)S(1)}, u32[]{:S(2)}, u32[]{:S(2)}) collective-permute-start(f32[32,1024]{1,0:T(8,128)S(1)} %select_add_fusion.2), channel_id=1, source_target_pairs={{0,16},{16,0},{1,17},{17,1},{2,18},{18,2},{3,19},{19,3},{4,20},{20... | collective-permute-start | bytes 393224 | tf_op jit(solution)/shard_map/ppermute | solution.py:347
  16.8 1.0 %collective-permute-done.2.swapped = f32[32,1024]{1,0:T(8,128)S(1)} collective-permute-done((f32[32,1024]{1,0:T(8,128)S(1)}, f32[32,1024]{1,0:T(8,128)S(1)}, u32[]{:S(2)}, u32[]{:S(2)}) %collective-permute-start.2) | collective-permute-done | bytes 131104 | tf_op jit(solution)/shard_map/ppermute | solution.py:347
  17.8 1.8 %middle.2 = (f32[32,1024]{1,0:T(8,128)S(1)}, f32[32,1024]{1,0:T(8,128)S(1)}, f32[4,32,1024]{2,1,0:T(8,128)S(1)}) custom-call(f32[32,1024]{1,0:T(8,128)S(1)} %add.18.kept, f32[32,1024]{1,0:T(8,128)S(1)} %collective-permute-done.1.crossed, f32[32,1024]{1,0:T(8,128)S(1)} %collective-permute-done.2.swapped, bf16[4,2,256,256]{3,2,1,0:T(8,128)(2,1)S(1)} %get-tuple-element.53.adj, ...), custom_call_target="tpu_custom_call" | custom-call | flops 838860800 | bytes 4194304 | tf_op jit(solution)/shard_map/middle/pallas_call | solution.py:307
  19.5 0.4 %collective-permute-start.3 = (f32[32,1024]{1,0:T(8,128)S(1)}, f32[32,1024]{1,0:T(8,128)S(1)}, u32[]{:S(2)}, u32[]{:S(2)}) collective-permute-start(f32[32,1024]{1,0:T(8,128)S(1)} %get-tuple-element.60), channel_id=1, source_target_pairs={{0,16},{16,0},{1,17},{17,1},{2,18},{18,2},{3,19},{19,3},{4,20},{20... | collective-permute-start | bytes 393224 | tf_op jit(solution)/shard_map/ppermute | solution.py:339
  20.0 1.0 %collective-permute-done.3 = f32[32,1024]{1,0:T(8,128)S(1)} collective-permute-done((f32[32,1024]{1,0:T(8,128)S(1)}, f32[32,1024]{1,0:T(8,128)S(1)}, u32[]{:S(2)}, u32[]{:S(2)}) %collective-permute-start.3) | collective-permute-done | bytes 131104 | tf_op jit(solution)/shard_map/ppermute | solution.py:339
  21.0 1.3 %collective-permute-start.4 = (f32[32,1024]{1,0:T(8,128)S(1)}, f32[32,1024]{1,0:T(8,128)S(1)}, u32[]{:S(2)}, u32[]{:S(2)}) collective-permute-start(f32[32,1024]{1,0:T(8,128)S(1)} %add.20.kept), channel_id=1, source_target_pairs={{0,1},{1,16},{2,3},{3,2},{4,5},{5,4},{6,7},{7,6},{8,9},{9,8},{10,1... | collective-permute-start | bytes 393224 | tf_op jit(solution)/shard_map/ppermute | solution.py:340
  22.2 0.8 %prepare.3 = (bf16[4,256,256]{2,1,0:T(8,128)(2,1)S(1)}, bf16[4,256,256]{2,1,0:T(8,128)(2,1)S(1)}, bf16[64,256]{1,0:T(8,128)(2,1)S(1)}, bf16[64,256]{1,0:T(8,128)...) custom-call(f32[4,16,128]{2,1,0:T(8,128)S(1)} %get-tuple-element.43.taps), custom_call_target="tpu_custom_call" | custom-call | flops 419430400 | bytes 4194304 | tf_op jit(solution)/shard_map/prepare/pallas_call | solution.py:307
  23.0 4.1 %collective-permute-done.4.crossed = f32[32,1024]{1,0:T(8,128)S(1)} collective-permute-done((f32[32,1024]{1,0:T(8,128)S(1)}, f32[32,1024]{1,0:T(8,128)S(1)}, u32[]{:S(2)}, u32[]{:S(2)}) %collective-permute-start.4) | collective-permute-done | bytes 131104 | tf_op jit(solution)/shard_map/ppermute | solution.py:340
  27.2 0.7 %collective-permute-start.5 = (f32[32,1024]{1,0:T(8,128)S(1)}, f32[32,1024]{1,0:T(8,128)S(1)}, u32[]{:S(2)}, u32[]{:S(2)}) collective-permute-start(f32[32,1024]{1,0:T(8,128)S(1)} %select_add_fusion.1), channel_id=1, source_target_pairs={{0,16},{16,0},{1,17},{17,1},{2,18},{18,2},{3,19},{19,3},{4,20},{20... | collective-permute-start | bytes 393224 | tf_op jit(solution)/shard_map/ppermute | solution.py:347
  27.9 1.0 %collective-permute-done.5.swapped = f32[32,1024]{1,0:T(8,128)S(1)} collective-permute-done((f32[32,1024]{1,0:T(8,128)S(1)}, f32[32,1024]{1,0:T(8,128)S(1)}, u32[]{:S(2)}, u32[]{:S(2)}) %collective-permute-start.5) | collective-permute-done | bytes 131104 | tf_op jit(solution)/shard_map/ppermute | solution.py:347
  28.8 1.8 %middle.3 = (f32[32,1024]{1,0:T(8,128)S(1)}, f32[32,1024]{1,0:T(8,128)S(1)}, f32[4,32,1024]{2,1,0:T(8,128)S(1)}) custom-call(f32[32,1024]{1,0:T(8,128)S(1)} %add.20.kept, f32[32,1024]{1,0:T(8,128)S(1)} %collective-permute-done.4.crossed, f32[32,1024]{1,0:T(8,128)S(1)} %collective-permute-done.5.swapped, bf16[4,2,256,256]{3,2,1,0:T(8,128)(2,1)S(1)} %get-tuple-element.68.adj, ...), custom_call_target="tpu_custom_call" | custom-call | flops 838860800 | bytes 4194304 | tf_op jit(solution)/shard_map/middle/pallas_call | solution.py:307
  30.6 0.4 %collective-permute-start.6 = (f32[32,1024]{1,0:T(8,128)S(1)}, f32[32,1024]{1,0:T(8,128)S(1)}, u32[]{:S(2)}, u32[]{:S(2)}) collective-permute-start(f32[32,1024]{1,0:T(8,128)S(1)} %get-tuple-element.76), channel_id=1, source_target_pairs={{0,16},{16,0},{1,17},{17,1},{2,18},{18,2},{3,19},{19,3},{4,20},{20... | collective-permute-start | bytes 393224 | tf_op jit(solution)/shard_map/ppermute | solution.py:339
  31.0 1.0 %collective-permute-done.6 = f32[32,1024]{1,0:T(8,128)S(1)} collective-permute-done((f32[32,1024]{1,0:T(8,128)S(1)}, f32[32,1024]{1,0:T(8,128)S(1)}, u32[]{:S(2)}, u32[]{:S(2)}) %collective-permute-start.6) | collective-permute-done | bytes 131104 | tf_op jit(solution)/shard_map/ppermute | solution.py:339
  32.1 1.2 %collective-permute-start.7 = (f32[32,1024]{1,0:T(8,128)S(1)}, f32[32,1024]{1,0:T(8,128)S(1)}, u32[]{:S(2)}, u32[]{:S(2)}) collective-permute-start(f32[32,1024]{1,0:T(8,128)S(1)} %add.22.kept), channel_id=1, source_target_pairs={{0,1},{1,16},{2,3},{3,2},{4,5},{5,4},{6,7},{7,6},{8,9},{9,8},{10,1... | collective-permute-start | bytes 393224 | tf_op jit(solution)/shard_map/ppermute | solution.py:340
  33.2 5.0 %collective-permute-done.7.crossed = f32[32,1024]{1,0:T(8,128)S(1)} collective-permute-done((f32[32,1024]{1,0:T(8,128)S(1)}, f32[32,1024]{1,0:T(8,128)S(1)}, u32[]{:S(2)}, u32[]{:S(2)}) %collective-permute-start.7) | collective-permute-done | bytes 131104 | tf_op jit(solution)/shard_map/ppermute | solution.py:340
  38.2 0.7 %collective-permute-start.8 = (f32[32,1024]{1,0:T(8,128)S(1)}, f32[32,1024]{1,0:T(8,128)S(1)}, u32[]{:S(2)}, u32[]{:S(2)}) collective-permute-start(f32[32,1024]{1,0:T(8,128)S(1)} %select_add_fusion), channel_id=1, source_target_pairs={{0,16},{16,0},{1,17},{17,1},{2,18},{18,2},{3,19},{19,3},{4,20},{20... | collective-permute-start | bytes 393224 | tf_op jit(solution)/shard_map/ppermute | solution.py:347
  38.9 1.0 %collective-permute-done.8.swapped = f32[32,1024]{1,0:T(8,128)S(1)} collective-permute-done((f32[32,1024]{1,0:T(8,128)S(1)}, f32[32,1024]{1,0:T(8,128)S(1)}, u32[]{:S(2)}, u32[]{:S(2)}) %collective-permute-start.8) | collective-permute-done | bytes 131104 | tf_op jit(solution)/shard_map/ppermute | solution.py:347
  39.9 1.6 %last.1 = (f32[4,32,1024]{2,1,0:T(8,128)}, f32[32,1024]{1,0:T(8,128)}) custom-call(f32[32,1024]{1,0:T(8,128)S(1)} %add.22.kept, f32[32,1024]{1,0:T(8,128)S(1)} %collective-permute-done.7.crossed, f32[32,1024]{1,0:T(8,128)S(1)} %collective-permute-done.8.swapped, bf16[4,2,256,256]{3,2,1,0:T(8,128)(2,1)S(1)} %get-tuple-element.77.adj, ...), custom_call_target="tpu_custom_call" | custom-call | flops 419430400 | bytes 4194304 | tf_op jit(solution)/shard_map/last/pallas_call | solution.py:307
  (14 shorter events, 0.1 us)
Async XLA Ops:
  0.6 0.7 %copy-start.6 = (s32[169,4]{0,1:T(4,128)S(1)}, s32[169,4]{0,1:T(4,128)}, u32[]{:S(2)}) copy-start(s32[169,4]{0,1:T(4,128)} %param.10) | copy-start | bytes 8116
  0.6 0.7 %copy-start.7 = (s32[3]{0:T(128)S(1)}, s32[3]{0:T(128)}, u32[]{:S(2)}) copy-start(s32[3]{0:T(128)} %view.1) | copy-start | bytes 40
  1.3 1.0 %copy-start = (f32[3,32,1024]{2,1,0:T(8,128)S(1)}, f32[3,32,1024]{2,1,0:T(8,128)}, u32[]{:S(2)}) copy-start(f32[3,32,1024]{2,1,0:T(8,128)} %measured.5) | copy-start | bytes 1179652
  2.3 1.0 %copy-start.2 = (f32[4,32,1024]{2,1,0:T(8,128)S(1)}, f32[4,32,1024]{2,1,0:T(8,128)}, u32[]{:S(2)}) copy-start(f32[4,32,1024]{2,1,0:T(8,128)} %volume.3) | copy-start | bytes 1572868
  3.4 0.9 %copy-start.4 = (f32[256,2,33]{0,1,2:T(2,128)S(1)}, f32[256,2,33]{0,1,2:T(2,128)}, u32[]{:S(2)}) copy-start(f32[256,2,33]{0,1,2:T(2,128)} %param.8) | copy-start | bytes 202756
  4.2 0.9 %copy-start.5 = (f32[256,2,33]{0,1,2:T(2,128)S(1)}, f32[256,2,33]{0,1,2:T(2,128)}, u32[]{:S(2)}) copy-start(f32[256,2,33]{0,1,2:T(2,128)} %param.9) | copy-start | bytes 202756
  8.2 1.7 %collective-permute-start = (f32[32,1024]{1,0:T(8,128)S(1)}, f32[32,1024]{1,0:T(8,128)S(1)}, u32[]{:S(2)}, u32[]{:S(2)}) collective-permute-start(f32[32,1024]{1,0:T(8,128)S(1)} %get-tuple-element.42), channel_id=1, source_target_pairs={{0,16},{16,0},{1,17},{17,1},{2,18},{18,2},{3,19},{19,3},{4,20},{20... | collective-permute-start | bytes 393224 | tf_op jit(solution)/shard_map/ppermute | solution.py:339
  9.9 5.3 %collective-permute-start.1 = (f32[32,1024]{1,0:T(8,128)S(1)}, f32[32,1024]{1,0:T(8,128)S(1)}, u32[]{:S(2)}, u32[]{:S(2)}) collective-permute-start(f32[32,1024]{1,0:T(8,128)S(1)} %add.18.kept), channel_id=1, source_target_pairs={{0,1},{1,16},{2,3},{3,2},{4,5},{5,4},{6,7},{7,6},{8,9},{9,8},{10,1... | collective-permute-start | bytes 393224 | tf_op jit(solution)/shard_map/ppermute | solution.py:340
  11.2 6.6 %copy-start.3 = (f32[4,32,1024]{2,1,0:T(8,128)S(1)}, f32[4,32,1024]{2,1,0:T(8,128)}, u32[]{:S(2)}) copy-start(f32[4,32,1024]{2,1,0:T(8,128)} %volume.3) | copy-start | bytes 1572868
  13.0 4.8 %copy-start.1 = (f32[3,32,1024]{2,1,0:T(8,128)S(1)}, f32[3,32,1024]{2,1,0:T(8,128)}, u32[]{:S(2)}) copy-start(f32[3,32,1024]{2,1,0:T(8,128)} %measured.5) | copy-start | bytes 1179652
  15.2 2.5 %collective-permute-start.2 = (f32[32,1024]{1,0:T(8,128)S(1)}, f32[32,1024]{1,0:T(8,128)S(1)}, u32[]{:S(2)}, u32[]{:S(2)}) collective-permute-start(f32[32,1024]{1,0:T(8,128)S(1)} %select_add_fusion.2), channel_id=1, source_target_pairs={{0,16},{16,0},{1,17},{17,1},{2,18},{18,2},{3,19},{19,3},{4,20},{20... | collective-permute-start | bytes 393224 | tf_op jit(solution)/shard_map/ppermute | solution.py:347
  19.5 1.4 %collective-permute-start.3 = (f32[32,1024]{1,0:T(8,128)S(1)}, f32[32,1024]{1,0:T(8,128)S(1)}, u32[]{:S(2)}, u32[]{:S(2)}) collective-permute-start(f32[32,1024]{1,0:T(8,128)S(1)} %get-tuple-element.60), channel_id=1, source_target_pairs={{0,16},{16,0},{1,17},{17,1},{2,18},{18,2},{3,19},{19,3},{4,20},{20... | collective-permute-start | bytes 393224 | tf_op jit(solution)/shard_map/ppermute | solution.py:339
  21.0 6.2 %collective-permute-start.4 = (f32[32,1024]{1,0:T(8,128)S(1)}, f32[32,1024]{1,0:T(8,128)S(1)}, u32[]{:S(2)}, u32[]{:S(2)}) collective-permute-start(f32[32,1024]{1,0:T(8,128)S(1)} %add.20.kept), channel_id=1, source_target_pairs={{0,1},{1,16},{2,3},{3,2},{4,5},{5,4},{6,7},{7,6},{8,9},{9,8},{10,1... | collective-permute-start | bytes 393224 | tf_op jit(solution)/shard_map/ppermute | solution.py:340
  27.2 1.7 %collective-permute-start.5 = (f32[32,1024]{1,0:T(8,128)S(1)}, f32[32,1024]{1,0:T(8,128)S(1)}, u32[]{:S(2)}, u32[]{:S(2)}) collective-permute-start(f32[32,1024]{1,0:T(8,128)S(1)} %select_add_fusion.1), channel_id=1, source_target_pairs={{0,16},{16,0},{1,17},{17,1},{2,18},{18,2},{3,19},{19,3},{4,20},{20... | collective-permute-start | bytes 393224 | tf_op jit(solution)/shard_map/ppermute | solution.py:347
  30.6 1.4 %collective-permute-start.6 = (f32[32,1024]{1,0:T(8,128)S(1)}, f32[32,1024]{1,0:T(8,128)S(1)}, u32[]{:S(2)}, u32[]{:S(2)}) collective-permute-start(f32[32,1024]{1,0:T(8,128)S(1)} %get-tuple-element.76), channel_id=1, source_target_pairs={{0,16},{16,0},{1,17},{17,1},{2,18},{18,2},{3,19},{19,3},{4,20},{20... | collective-permute-start | bytes 393224 | tf_op jit(solution)/shard_map/ppermute | solution.py:339
  32.1 6.2 %collective-permute-start.7 = (f32[32,1024]{1,0:T(8,128)S(1)}, f32[32,1024]{1,0:T(8,128)S(1)}, u32[]{:S(2)}, u32[]{:S(2)}) collective-permute-start(f32[32,1024]{1,0:T(8,128)S(1)} %add.22.kept), channel_id=1, source_target_pairs={{0,1},{1,16},{2,3},{3,2},{4,5},{5,4},{6,7},{7,6},{8,9},{9,8},{10,1... | collective-permute-start | bytes 393224 | tf_op jit(solution)/shard_map/ppermute | solution.py:340
  38.2 1.7 %collective-permute-start.8 = (f32[32,1024]{1,0:T(8,128)S(1)}, f32[32,1024]{1,0:T(8,128)S(1)}, u32[]{:S(2)}, u32[]{:S(2)}) collective-permute-start(f32[32,1024]{1,0:T(8,128)S(1)} %select_add_fusion), channel_id=1, source_target_pairs={{0,16},{16,0},{1,17},{17,1},{2,18},{18,2},{3,19},{19,3},{4,20},{20... | collective-permute-start | bytes 393224 | tf_op jit(solution)/shard_map/ppermute | solution.py:347
where the time goes:
time: 42.1 us; the launch traced here: 41.6 us
  waiting for transfers between devices  17.2 us (41%)
  Pallas kernels  10.8 us (26%)
  starting transfers between devices  8.21 us (20%)
  local copies, waits for them, and re-layouts  4.48 us (11%)
  between operations  0.72 us (2%)
    ppermute x3, waiting for transfers between devices, exchange(): lax.ppermute(kept, ('depth', 'tile'), [(i, flow(i)) for i in range(2 * ti...  11.3 us
    pallas_call x6, Pallas kernels, call(): pl.pallas_call(kernel, out_shape=outs, in_specs=in_specs, out_specs=out_s...  10.8 us
    unnamed x16, local copies, waits for them, and re-layouts  4.48 us
    ppermute x3, starting transfers between devices, exchange(): lax.ppermute(kept, ('depth', 'tile'), [(i, flow(i)) for i in range(2 * ti...  3.68 us
    ppermute x3, waiting for transfers between devices, exchange(): return (kept, crossed, lax.ppermute(send, 'depth', swap), ready)  2.96 us
    ppermute x3, waiting for transfers between devices, exchange(): kept = mine + lax.ppermute(other, 'depth', swap)  2.96 us
    ppermute x3, starting transfers between devices, exchange(): return (kept, crossed, lax.ppermute(send, 'depth', swap), ready)  2.93 us
    ppermute x3, starting transfers between devices, exchange(): kept = mine + lax.ppermute(other, 'depth', swap)  1.6 us
  transfers between devices with their start and end apart: 9, of which 9 were waited for; matrix products, arithmetic and copies ran while one was open for 0% of the time, Pallas kernels for 6%

commit v1 on v0

--- a/solution.py
+++ b/solution.py
@@ -208,12 +208,12 @@
 
 
 def first_kernel(
-    paired, view, index, row_bank, col_bank, volume, measured, mine, other, taps,
-    index_v, row_v, col_v, volume_v, measured_v, fwd_hi, fwd_lo, w_hi, w_lo, sems,
+    paired, view_h, index, row_bank, col_bank, volume, measured, mine, other, taps,
+    view, index_v, row_v, col_v, volume_v, measured_v, fwd_hi, fwd_lo, w_hi, w_lo, sems,
 ):
     pairs = [
-        (index, index_v), (col_bank, col_v), (row_bank, row_v), (volume, volume_v),
-        (measured.at[0], measured_v),
+        (view_h, view), (index, index_v), (col_bank, col_v), (row_bank, row_v),
+        (volume, volume_v), (measured.at[0], measured_v),
     ]
     copies = [pltpu.make_async_copy(a, b, sems.at[i]) for i, (a, b) in enumerate(pairs)]
     for copy in copies:
@@ -221,13 +221,13 @@
     place = Place(paired)
     planes = volume.shape[0]
     reach = (row_bank.shape[0] - 1) // 2
-    for copy in copies[:3]:
+    for copy in copies[:4]:
         copy.wait()
     pick_taps(view.shape[0], planes, view, index_v[...], (row_v, col_v), taps)
     for d in range(planes):
         column_operands(taps, d, d, reach, (fwd_hi, fwd_lo), None)
     row_hi, row_lo = split(row_operand(taps, 0, planes, reach, place))
-    for copy in copies[3:]:
+    for copy in copies[4:]:
         copy.wait()
     target = window_target(measured_v[...], place) if paired else 0.0
     mine[...], other[...] = forward(
@@ -299,7 +299,6 @@
 
 
 VMEM = pl.BlockSpec(memory_space=pltpu.VMEM)
-SMEM = pl.BlockSpec(memory_space=pltpu.SMEM)
 HBM = pl.BlockSpec(memory_space=pltpu.HBM)
 
 
@@ -379,12 +378,15 @@
     index = kernel_index.T
     banks = [jnp.transpose(x, (2, 1, 0)) for x in (row_bank, col_bank)]
     mine, other, taps = call(
-        functools.partial(first_kernel, paired), [SMEM] + [HBM] * 5, [VMEM] * 3,
+        functools.partial(first_kernel, paired), [HBM] * 6, [VMEM] * 3,
         [image, image, tap_shape],
-        [pltpu.VMEM(x.shape, x.dtype) for x in (index, *banks, volume, measured[0])]
+        [pltpu.SMEM(view_order.shape, jnp.int32)]
+        + [pltpu.VMEM(x.shape, x.dtype) for x in (index, *banks, volume, measured[0])]
         + [pltpu.VMEM(x.shape, x.dtype) for x in forward_shapes[:2]]
-        + scratch + [pltpu.SemaphoreType.DMA((5,))],
-        work, "first", (view_order, index, *banks, volume, measured),
+        + scratch + [pltpu.SemaphoreType.DMA((6,))],
+        work, "first",
+        [pltpu.with_memory_space_constraint(x, pltpu.HBM)
+         for x in (view_order, index, *banks, volume, measured)],
     )
 
     def prepare(back, ahead):

time: 42.1 us -> 37.4 us (0.89)
  local copies, waits for them, and re-layouts: 4.48 us -> 0.01 us
    unnamed x16 -> x4, local copies, waits for them, and re-layouts: 4.48 us -> 0.01 us
  transfers between devices with their start and end apart: 9 -> 9, of which waited for: 9 -> 9; matrix products, arithmetic and copies ran while one was open for 0% -> 0% of each run, Pallas kernels for 6% -> 7%
where the time goes in v1:
time: 37.4 us; the launch traced here: 37.1 us
  waiting for transfers between devices  17.2 us (46%)
  Pallas kernels  10.8 us (29%)
  starting transfers between devices  8.22 us (22%)
  between operations  0.7 us (2%)
    ppermute x3, waiting for transfers between devices, exchange(): lax.ppermute(kept, ('depth', 'tile'), [(i, flow(i)) for i in range(2 * ti...  11.3 us
    pallas_call x6, Pallas kernels, call(): pl.pallas_call(kernel, out_shape=outs, in_specs=in_specs, out_specs=out_s...  10.8 us
    ppermute x3, starting transfers between devices, exchange(): lax.ppermute(kept, ('depth', 'tile'), [(i, flow(i)) for i in range(2 * ti...  3.68 us
    ppermute x3, waiting for transfers between devices, exchange(): kept = mine + lax.ppermute(other, 'depth', swap)  2.96 us
    ppermute x3, waiting for transfers between devices, exchange(): return (kept, crossed, lax.ppermute(send, 'depth', swap), ready)  2.96 us
    ppermute x3, starting transfers between devices, exchange(): return (kept, crossed, lax.ppermute(send, 'depth', swap), ready)  2.94 us
    ppermute x3, starting transfers between devices, exchange(): kept = mine + lax.ppermute(other, 'depth', swap)  1.59 us
  transfers between devices with their start and end apart: 9, of which 9 were waited for; matrix products, arithmetic and copies ran while one was open for 0% of the time, Pallas kernels for 7%

profile of v1, /device:TPU:11, one launch (start us, length us, event | category | flops | bytes accessed | tf_op | source)
XLA Modules:
  0.0 37.1 jit_solution(8203559977868214489)
XLA Ops:
  0.6 3.0 %first.1 = (f32[32,1024]{1,0:T(8,128)S(1)}, f32[32,1024]{1,0:T(8,128)S(1)}, f32[4,16,128]{2,1,0:T(8,128)S(1)}) custom-call(s32[3]{0:T(128)} %view_h.1, s32[4,169]{1,0:T(4,128)} %bitcast.5, f32[33,2,256]{2,1,0:T(2,128)} %bitcast.3, f32[33,2,256]{2,1,0:T(2,128)} %bitcast.4, f32[4,32,1024]{2,1,0:T(8,128)} %volume.3, f32[3,32,1024]{2,1,0:T(8,128)} %measured.5), custom_call_target="tpu_custom_call" | custom-call | flops 419430400 | bytes 4194304 | tf_op jit(solution)/shard_map/first/pallas_call | solution.py:306
  3.7 0.7 %collective-permute-start = (f32[32,1024]{1,0:T(8,128)S(1)}, f32[32,1024]{1,0:T(8,128)S(1)}, u32[]{:S(2)}, u32[]{:S(2)}) collective-permute-start(f32[32,1024]{1,0:T(8,128)S(1)} %get-tuple-element.42), channel_id=1, source_target_pairs={{0,16},{16,0},{1,17},{17,1},{2,18},{18,2},{3,19},{19,3},{4,20},{20... | collective-permute-start | bytes 393224 | tf_op jit(solution)/shard_map/ppermute | solution.py:338
  4.4 1.0 %collective-permute-done = f32[32,1024]{1,0:T(8,128)S(1)} collective-permute-done((f32[32,1024]{1,0:T(8,128)S(1)}, f32[32,1024]{1,0:T(8,128)S(1)}, u32[]{:S(2)}, u32[]{:S(2)}) %collective-permute-start) | collective-permute-done | bytes 131104 | tf_op jit(solution)/shard_map/ppermute | solution.py:338
  5.4 1.3 %collective-permute-start.1 = (f32[32,1024]{1,0:T(8,128)S(1)}, f32[32,1024]{1,0:T(8,128)S(1)}, u32[]{:S(2)}, u32[]{:S(2)}) collective-permute-start(f32[32,1024]{1,0:T(8,128)S(1)} %add.18.kept), channel_id=1, source_target_pairs={{0,1},{1,16},{2,3},{3,2},{4,5},{5,4},{6,7},{7,6},{8,9},{9,8},{10,1... | collective-permute-start | bytes 393224 | tf_op jit(solution)/shard_map/ppermute | solution.py:339
  6.7 0.0 copy-start.1
  6.7 1.8 %prepare.2 = (bf16[4,256,256]{2,1,0:T(8,128)(2,1)S(1)}, bf16[4,256,256]{2,1,0:T(8,128)(2,1)S(1)}, bf16[64,256]{1,0:T(8,128)(2,1)S(1)}, bf16[64,256]{1,0:T(8,128)...) custom-call(f32[4,16,128]{2,1,0:T(8,128)S(1)} %get-tuple-element.43.taps), custom_call_target="tpu_custom_call" | custom-call | flops 419430400 | bytes 4194304 | tf_op jit(solution)/shard_map/prepare/pallas_call | solution.py:306
  8.5 0.0 copy-start
  8.5 2.2 %collective-permute-done.1.crossed = f32[32,1024]{1,0:T(8,128)S(1)} collective-permute-done((f32[32,1024]{1,0:T(8,128)S(1)}, f32[32,1024]{1,0:T(8,128)S(1)}, u32[]{:S(2)}, u32[]{:S(2)}) %collective-permute-start.1) | collective-permute-done | bytes 131104 | tf_op jit(solution)/shard_map/ppermute | solution.py:339
  10.7 1.6 %collective-permute-start.2 = (f32[32,1024]{1,0:T(8,128)S(1)}, f32[32,1024]{1,0:T(8,128)S(1)}, u32[]{:S(2)}, u32[]{:S(2)}) collective-permute-start(f32[32,1024]{1,0:T(8,128)S(1)} %select_add_fusion.2), channel_id=1, source_target_pairs={{0,16},{16,0},{1,17},{17,1},{2,18},{18,2},{3,19},{19,3},{4,20},{20... | collective-permute-start | bytes 393224 | tf_op jit(solution)/shard_map/ppermute | solution.py:346
  12.3 1.0 %collective-permute-done.2.swapped = f32[32,1024]{1,0:T(8,128)S(1)} collective-permute-done((f32[32,1024]{1,0:T(8,128)S(1)}, f32[32,1024]{1,0:T(8,128)S(1)}, u32[]{:S(2)}, u32[]{:S(2)}) %collective-permute-start.2) | collective-permute-done | bytes 131104 | tf_op jit(solution)/shard_map/ppermute | solution.py:346
  13.3 0.0 copy-done.1
  13.3 0.0 copy-done
  13.3 1.8 %middle.2 = (f32[32,1024]{1,0:T(8,128)S(1)}, f32[32,1024]{1,0:T(8,128)S(1)}, f32[4,32,1024]{2,1,0:T(8,128)S(1)}) custom-call(f32[32,1024]{1,0:T(8,128)S(1)} %add.18.kept, f32[32,1024]{1,0:T(8,128)S(1)} %collective-permute-done.1.crossed, f32[32,1024]{1,0:T(8,128)S(1)} %collective-permute-done.2.swapped, bf16[4,2,256,256]{3,2,1,0:T(8,128)(2,1)S(1)} %get-tuple-element.53.adj, ...), custom_call_target="tpu_custom_call" | custom-call | flops 838860800 | bytes 4194304 | tf_op jit(solution)/shard_map/middle/pallas_call | solution.py:306
  15.1 0.4 %collective-permute-start.3 = (f32[32,1024]{1,0:T(8,128)S(1)}, f32[32,1024]{1,0:T(8,128)S(1)}, u32[]{:S(2)}, u32[]{:S(2)}) collective-permute-start(f32[32,1024]{1,0:T(8,128)S(1)} %get-tuple-element.60), channel_id=1, source_target_pairs={{0,16},{16,0},{1,17},{17,1},{2,18},{18,2},{3,19},{19,3},{4,20},{20... | collective-permute-start | bytes 393224 | tf_op jit(solution)/shard_map/ppermute | solution.py:338
  15.5 1.0 %collective-permute-done.3 = f32[32,1024]{1,0:T(8,128)S(1)} collective-permute-done((f32[32,1024]{1,0:T(8,128)S(1)}, f32[32,1024]{1,0:T(8,128)S(1)}, u32[]{:S(2)}, u32[]{:S(2)}) %collective-permute-start.3) | collective-permute-done | bytes 131104 | tf_op jit(solution)/shard_map/ppermute | solution.py:338
  16.5 1.3 %collective-permute-start.4 = (f32[32,1024]{1,0:T(8,128)S(1)}, f32[32,1024]{1,0:T(8,128)S(1)}, u32[]{:S(2)}, u32[]{:S(2)}) collective-permute-start(f32[32,1024]{1,0:T(8,128)S(1)} %add.20.kept), channel_id=1, source_target_pairs={{0,1},{1,16},{2,3},{3,2},{4,5},{5,4},{6,7},{7,6},{8,9},{9,8},{10,1... | collective-permute-start | bytes 393224 | tf_op jit(solution)/shard_map/ppermute | solution.py:339
  17.8 0.8 %prepare.3 = (bf16[4,256,256]{2,1,0:T(8,128)(2,1)S(1)}, bf16[4,256,256]{2,1,0:T(8,128)(2,1)S(1)}, bf16[64,256]{1,0:T(8,128)(2,1)S(1)}, bf16[64,256]{1,0:T(8,128)...) custom-call(f32[4,16,128]{2,1,0:T(8,128)S(1)} %get-tuple-element.43.taps), custom_call_target="tpu_custom_call" | custom-call | flops 419430400 | bytes 4194304 | tf_op jit(solution)/shard_map/prepare/pallas_call | solution.py:306
  18.5 4.1 %collective-permute-done.4.crossed = f32[32,1024]{1,0:T(8,128)S(1)} collective-permute-done((f32[32,1024]{1,0:T(8,128)S(1)}, f32[32,1024]{1,0:T(8,128)S(1)}, u32[]{:S(2)}, u32[]{:S(2)}) %collective-permute-start.4) | collective-permute-done | bytes 131104 | tf_op jit(solution)/shard_map/ppermute | solution.py:339
  22.7 0.7 %collective-permute-start.5 = (f32[32,1024]{1,0:T(8,128)S(1)}, f32[32,1024]{1,0:T(8,128)S(1)}, u32[]{:S(2)}, u32[]{:S(2)}) collective-permute-start(f32[32,1024]{1,0:T(8,128)S(1)} %select_add_fusion.1), channel_id=1, source_target_pairs={{0,16},{16,0},{1,17},{17,1},{2,18},{18,2},{3,19},{19,3},{4,20},{20... | collective-permute-start | bytes 393224 | tf_op jit(solution)/shard_map/ppermute | solution.py:346
  23.4 1.0 %collective-permute-done.5.swapped = f32[32,1024]{1,0:T(8,128)S(1)} collective-permute-done((f32[32,1024]{1,0:T(8,128)S(1)}, f32[32,1024]{1,0:T(8,128)S(1)}, u32[]{:S(2)}, u32[]{:S(2)}) %collective-permute-start.5) | collective-permute-done | bytes 131104 | tf_op jit(solution)/shard_map/ppermute | solution.py:346
  24.4 1.8 %middle.3 = (f32[32,1024]{1,0:T(8,128)S(1)}, f32[32,1024]{1,0:T(8,128)S(1)}, f32[4,32,1024]{2,1,0:T(8,128)S(1)}) custom-call(f32[32,1024]{1,0:T(8,128)S(1)} %add.20.kept, f32[32,1024]{1,0:T(8,128)S(1)} %collective-permute-done.4.crossed, f32[32,1024]{1,0:T(8,128)S(1)} %collective-permute-done.5.swapped, bf16[4,2,256,256]{3,2,1,0:T(8,128)(2,1)S(1)} %get-tuple-element.68.adj, ...), custom_call_target="tpu_custom_call" | custom-call | flops 838860800 | bytes 4194304 | tf_op jit(solution)/shard_map/middle/pallas_call | solution.py:306
  26.1 0.4 %collective-permute-start.6 = (f32[32,1024]{1,0:T(8,128)S(1)}, f32[32,1024]{1,0:T(8,128)S(1)}, u32[]{:S(2)}, u32[]{:S(2)}) collective-permute-start(f32[32,1024]{1,0:T(8,128)S(1)} %get-tuple-element.76), channel_id=1, source_target_pairs={{0,16},{16,0},{1,17},{17,1},{2,18},{18,2},{3,19},{19,3},{4,20},{20... | collective-permute-start | bytes 393224 | tf_op jit(solution)/shard_map/ppermute | solution.py:338
  26.6 1.0 %collective-permute-done.6 = f32[32,1024]{1,0:T(8,128)S(1)} collective-permute-done((f32[32,1024]{1,0:T(8,128)S(1)}, f32[32,1024]{1,0:T(8,128)S(1)}, u32[]{:S(2)}, u32[]{:S(2)}) %collective-permute-start.6) | collective-permute-done | bytes 131104 | tf_op jit(solution)/shard_map/ppermute | solution.py:338
  27.6 1.1 %collective-permute-start.7 = (f32[32,1024]{1,0:T(8,128)S(1)}, f32[32,1024]{1,0:T(8,128)S(1)}, u32[]{:S(2)}, u32[]{:S(2)}) collective-permute-start(f32[32,1024]{1,0:T(8,128)S(1)} %add.22.kept), channel_id=1, source_target_pairs={{0,1},{1,16},{2,3},{3,2},{4,5},{5,4},{6,7},{7,6},{8,9},{9,8},{10,1... | collective-permute-start | bytes 393224 | tf_op jit(solution)/shard_map/ppermute | solution.py:339
  28.7 5.0 %collective-permute-done.7.crossed = f32[32,1024]{1,0:T(8,128)S(1)} collective-permute-done((f32[32,1024]{1,0:T(8,128)S(1)}, f32[32,1024]{1,0:T(8,128)S(1)}, u32[]{:S(2)}, u32[]{:S(2)}) %collective-permute-start.7) | collective-permute-done | bytes 131104 | tf_op jit(solution)/shard_map/ppermute | solution.py:339
  33.8 0.7 %collective-permute-start.8 = (f32[32,1024]{1,0:T(8,128)S(1)}, f32[32,1024]{1,0:T(8,128)S(1)}, u32[]{:S(2)}, u32[]{:S(2)}) collective-permute-start(f32[32,1024]{1,0:T(8,128)S(1)} %select_add_fusion), channel_id=1, source_target_pairs={{0,16},{16,0},{1,17},{17,1},{2,18},{18,2},{3,19},{19,3},{4,20},{20... | collective-permute-start | bytes 393224 | tf_op jit(solution)/shard_map/ppermute | solution.py:346
  34.4 1.0 %collective-permute-done.8.swapped = f32[32,1024]{1,0:T(8,128)S(1)} collective-permute-done((f32[32,1024]{1,0:T(8,128)S(1)}, f32[32,1024]{1,0:T(8,128)S(1)}, u32[]{:S(2)}, u32[]{:S(2)}) %collective-permute-start.8) | collective-permute-done | bytes 131104 | tf_op jit(solution)/shard_map/ppermute | solution.py:346
  35.4 1.6 %last.1 = (f32[4,32,1024]{2,1,0:T(8,128)}, f32[32,1024]{1,0:T(8,128)}) custom-call(f32[32,1024]{1,0:T(8,128)S(1)} %add.22.kept, f32[32,1024]{1,0:T(8,128)S(1)} %collective-permute-done.7.crossed, f32[32,1024]{1,0:T(8,128)S(1)} %collective-permute-done.8.swapped, bf16[4,2,256,256]{3,2,1,0:T(8,128)(2,1)S(1)} %get-tuple-element.77.adj, ...), custom_call_target="tpu_custom_call" | custom-call | flops 419430400 | bytes 4194304 | tf_op jit(solution)/shard_map/last/pallas_call | solution.py:306
  (6 shorter events, 0.1 us)
Async XLA Ops:
  3.7 1.7 %collective-permute-start = (f32[32,1024]{1,0:T(8,128)S(1)}, f32[32,1024]{1,0:T(8,128)S(1)}, u32[]{:S(2)}, u32[]{:S(2)}) collective-permute-start(f32[32,1024]{1,0:T(8,128)S(1)} %get-tuple-element.42), channel_id=1, source_target_pairs={{0,16},{16,0},{1,17},{17,1},{2,18},{18,2},{3,19},{19,3},{4,20},{20... | collective-permute-start | bytes 393224 | tf_op jit(solution)/shard_map/ppermute | solution.py:338
  5.4 5.3 %collective-permute-start.1 = (f32[32,1024]{1,0:T(8,128)S(1)}, f32[32,1024]{1,0:T(8,128)S(1)}, u32[]{:S(2)}, u32[]{:S(2)}) collective-permute-start(f32[32,1024]{1,0:T(8,128)S(1)} %add.18.kept), channel_id=1, source_target_pairs={{0,1},{1,16},{2,3},{3,2},{4,5},{5,4},{6,7},{7,6},{8,9},{9,8},{10,1... | collective-permute-start | bytes 393224 | tf_op jit(solution)/shard_map/ppermute | solution.py:339
  6.7 6.6 %copy-start.1 = (f32[4,32,1024]{2,1,0:T(8,128)S(1)}, f32[4,32,1024]{2,1,0:T(8,128)}, u32[]{:S(2)}) copy-start(f32[4,32,1024]{2,1,0:T(8,128)} %volume.3) | copy-start | bytes 1572868
  8.5 4.8 %copy-start = (f32[3,32,1024]{2,1,0:T(8,128)S(1)}, f32[3,32,1024]{2,1,0:T(8,128)}, u32[]{:S(2)}) copy-start(f32[3,32,1024]{2,1,0:T(8,128)} %measured.5) | copy-start | bytes 1179652
  10.7 2.6 %collective-permute-start.2 = (f32[32,1024]{1,0:T(8,128)S(1)}, f32[32,1024]{1,0:T(8,128)S(1)}, u32[]{:S(2)}, u32[]{:S(2)}) collective-permute-start(f32[32,1024]{1,0:T(8,128)S(1)} %select_add_fusion.2), channel_id=1, source_target_pairs={{0,16},{16,0},{1,17},{17,1},{2,18},{18,2},{3,19},{19,3},{4,20},{20... | collective-permute-start | bytes 393224 | tf_op jit(solution)/shard_map/ppermute | solution.py:346
  15.1 1.4 %collective-permute-start.3 = (f32[32,1024]{1,0:T(8,128)S(1)}, f32[32,1024]{1,0:T(8,128)S(1)}, u32[]{:S(2)}, u32[]{:S(2)}) collective-permute-start(f32[32,1024]{1,0:T(8,128)S(1)} %get-tuple-element.60), channel_id=1, source_target_pairs={{0,16},{16,0},{1,17},{17,1},{2,18},{18,2},{3,19},{19,3},{4,20},{20... | collective-permute-start | bytes 393224 | tf_op jit(solution)/shard_map/ppermute | solution.py:338
  16.5 6.1 %collective-permute-start.4 = (f32[32,1024]{1,0:T(8,128)S(1)}, f32[32,1024]{1,0:T(8,128)S(1)}, u32[]{:S(2)}, u32[]{:S(2)}) collective-permute-start(f32[32,1024]{1,0:T(8,128)S(1)} %add.20.kept), channel_id=1, source_target_pairs={{0,1},{1,16},{2,3},{3,2},{4,5},{5,4},{6,7},{7,6},{8,9},{9,8},{10,1... | collective-permute-start | bytes 393224 | tf_op jit(solution)/shard_map/ppermute | solution.py:339
  22.7 1.7 %collective-permute-start.5 = (f32[32,1024]{1,0:T(8,128)S(1)}, f32[32,1024]{1,0:T(8,128)S(1)}, u32[]{:S(2)}, u32[]{:S(2)}) collective-permute-start(f32[32,1024]{1,0:T(8,128)S(1)} %select_add_fusion.1), channel_id=1, source_target_pairs={{0,16},{16,0},{1,17},{17,1},{2,18},{18,2},{3,19},{19,3},{4,20},{20... | collective-permute-start | bytes 393224 | tf_op jit(solution)/shard_map/ppermute | solution.py:346
  26.1 1.4 %collective-permute-start.6 = (f32[32,1024]{1,0:T(8,128)S(1)}, f32[32,1024]{1,0:T(8,128)S(1)}, u32[]{:S(2)}, u32[]{:S(2)}) collective-permute-start(f32[32,1024]{1,0:T(8,128)S(1)} %get-tuple-element.76), channel_id=1, source_target_pairs={{0,16},{16,0},{1,17},{17,1},{2,18},{18,2},{3,19},{19,3},{4,20},{20... | collective-permute-start | bytes 393224 | tf_op jit(solution)/shard_map/ppermute | solution.py:338
  27.6 6.2 %collective-permute-start.7 = (f32[32,1024]{1,0:T(8,128)S(1)}, f32[32,1024]{1,0:T(8,128)S(1)}, u32[]{:S(2)}, u32[]{:S(2)}) collective-permute-start(f32[32,1024]{1,0:T(8,128)S(1)} %add.22.kept), channel_id=1, source_target_pairs={{0,1},{1,16},{2,3},{3,2},{4,5},{5,4},{6,7},{7,6},{8,9},{9,8},{10,1... | collective-permute-start | bytes 393224 | tf_op jit(solution)/shard_map/ppermute | solution.py:339
  33.8 1.7 %collective-permute-start.8 = (f32[32,1024]{1,0:T(8,128)S(1)}, f32[32,1024]{1,0:T(8,128)S(1)}, u32[]{:S(2)}, u32[]{:S(2)}) collective-permute-start(f32[32,1024]{1,0:T(8,128)S(1)} %select_add_fusion), channel_id=1, source_target_pairs={{0,16},{16,0},{1,17},{17,1},{2,18},{18,2},{3,19},{19,3},{4,20},{20... | collective-permute-start | bytes 393224 | tf_op jit(solution)/shard_map/ppermute | solution.py:346

commit v2 on v1

--- a/solution.py
+++ b/solution.py
@@ -42,10 +42,12 @@
         odd = lax.rem(t, 2)
         self.first = t == 0
         self.last = t == tiles - 1
-        self.flag = 1 - jnp.bitwise_xor(odd, d) if paired else 1 - odd
-        end = jnp.logical_and(jnp.logical_or(self.first, self.last), paired)
-        self.end_even = jnp.logical_and(end, d == 0)
-        self.end_odd = jnp.logical_and(end, d == 1)
+        end = jnp.logical_or(self.first, self.last)
+        side = jnp.where(end, 1 - d, d)
+        self.flag = 1 - jnp.bitwise_xor(odd, side) if paired else 1 - odd
+        end = jnp.logical_and(end, paired)
+        self.end_even = jnp.logical_and(end, side == 0)
+        self.end_odd = jnp.logical_and(end, side == 1)
 
 
 def pick_taps(steps, planes, view_ref, index, banks, taps_ref):
@@ -62,15 +64,15 @@
     taps_ref[...] = jnp.zeros(taps_ref.shape, f32)
     for b, bank in enumerate(banks):
         for r in range(2):
-            hi, lo = split(bank[:, r, :])
+            hi, lo = split(bank[r])
             taps = dot_nt(chosen, hi) + dot_nt(chosen, lo)
             taps_ref[2 * b + r, :, 0 : taps.shape[1]] = taps
 
 
 def column_operands(taps_ref, line, d, reach, forward_out, adjoint_out):
     square = (LANES, LANES)
-    below = lane_iota(square) < row_iota(square)
-    above = lane_iota(square) > row_iota(square)
+    below = (lane_iota(square) < row_iota(square)).astype(f32).astype(bf16)
+    above = (lane_iota(square) > row_iota(square)).astype(f32).astype(bf16)
     for r in range(2):
         base = pltpu.roll(
             jnp.broadcast_to(taps_ref[2 + r, line : line + 1], (8, LANES)),
@@ -79,8 +81,8 @@
         ring = jnp.concatenate(
             [base] + [pltpu.roll(base, 8 * b, 1) for b in range(1, LANES // 8)], axis=0
         )
-        low_hi, low_lo = split(jnp.where(below, ring, 0.0))
-        up_hi, up_lo = split(jnp.where(above, ring, 0.0))
+        hi, lo = split(ring)
+        low_hi, low_lo, up_hi, up_lo = hi * below, lo * below, hi * above, lo * above
         left, right = slice(0, LANES), slice(LANES, 2 * LANES)
         if forward_out is not None:
             fwd_hi, fwd_lo = forward_out
@@ -211,23 +213,22 @@
     paired, view_h, index, row_bank, col_bank, volume, measured, mine, other, taps,
     view, index_v, row_v, col_v, volume_v, measured_v, fwd_hi, fwd_lo, w_hi, w_lo, sems,
 ):
-    pairs = [
-        (view_h, view), (index, index_v), (col_bank, col_v), (row_bank, row_v),
-        (volume, volume_v), (measured.at[0], measured_v),
-    ]
+    pairs = [(view_h, view), (index, index_v)]
+    pairs += [(b.at[:, r, :], v.at[r]) for b, v in ((col_bank, col_v), (row_bank, row_v)) for r in range(2)]
+    pairs += [(volume, volume_v), (measured.at[0], measured_v)]
     copies = [pltpu.make_async_copy(a, b, sems.at[i]) for i, (a, b) in enumerate(pairs)]
     for copy in copies:
         copy.start()
     place = Place(paired)
     planes = volume.shape[0]
     reach = (row_bank.shape[0] - 1) // 2
-    for copy in copies[:4]:
+    for copy in copies[:6]:
         copy.wait()
     pick_taps(view.shape[0], planes, view, index_v[...], (row_v, col_v), taps)
     for d in range(planes):
         column_operands(taps, d, d, reach, (fwd_hi, fwd_lo), None)
     row_hi, row_lo = split(row_operand(taps, 0, planes, reach, place))
-    for copy in copies[4:]:
+    for copy in copies[6:]:
         copy.wait()
     target = window_target(measured_v[...], place) if paired else 0.0
     mine[...], other[...] = forward(
@@ -327,10 +328,9 @@
 
     def flow(spot):
         side, i = divmod(spot, tiles)
-        ends = (0, tiles - 1)
-        if side == 1:
-            return i if i in ends else tiles + (i + 1 if i % 2 else i - 1)
-        return tiles + (i ^ 1) if (i ^ 1) in ends else i ^ 1
+        if i in (0, tiles - 1):
+            return i ^ 1 if side else tiles + i
+        return tiles + (i + 1 if i % 2 else i - 1) if side else i ^ 1
 
     def exchange(mine, other, step, during):
         if paired:
@@ -381,9 +381,11 @@
         functools.partial(first_kernel, paired), [HBM] * 6, [VMEM] * 3,
         [image, image, tap_shape],
         [pltpu.SMEM(view_order.shape, jnp.int32)]
-        + [pltpu.VMEM(x.shape, x.dtype) for x in (index, *banks, volume, measured[0])]
+        + [pltpu.VMEM(index.shape, index.dtype)]
+        + [pltpu.VMEM((2, x.shape[0], x.shape[2]), f32) for x in banks]
+        + [pltpu.VMEM(x.shape, f32) for x in (volume, measured[0])]
         + [pltpu.VMEM(x.shape, x.dtype) for x in forward_shapes[:2]]
-        + scratch + [pltpu.SemaphoreType.DMA((6,))],
+        + scratch + [pltpu.SemaphoreType.DMA((8,))],
         work, "first",
         [pltpu.with_memory_space_constraint(x, pltpu.HBM)
          for x in (view_order, index, *banks, volume, measured)],

time: 37.4 us -> 36.9 us (0.987)
  no operation moved by 1% of the time
where the time goes in v2:
time: 36.9 us; the launch traced here: 36.7 us
  waiting for transfers between devices  17.2 us (47%)
  Pallas kernels  10.5 us (28%)
  starting transfers between devices  8.2 us (22%)
  between operations  0.7 us (2%)
    ppermute x3, waiting for transfers between devices, exchange(): lax.ppermute(kept, ('depth', 'tile'), [(i, flow(i)) for i in range(2 * ti...  11.3 us
    pallas_call x6, Pallas kernels, call(): pl.pallas_call(kernel, out_shape=outs, in_specs=in_specs, out_specs=out_s...  10.5 us
    ppermute x3, starting transfers between devices, exchange(): lax.ppermute(kept, ('depth', 'tile'), [(i, flow(i)) for i in range(2 * ti...  3.67 us
    ppermute x3, waiting for transfers between devices, exchange(): kept = mine + lax.ppermute(other, 'depth', swap)  2.96 us
    ppermute x3, waiting for transfers between devices, exchange(): return (kept, crossed, lax.ppermute(send, 'depth', swap), ready)  2.96 us
    ppermute x3, starting transfers between devices, exchange(): return (kept, crossed, lax.ppermute(send, 'depth', swap), ready)  2.94 us
    ppermute x3, starting transfers between devices, exchange(): kept = mine + lax.ppermute(other, 'depth', swap)  1.6 us
  transfers between devices with their start and end apart: 9, of which 9 were waited for; matrix products, arithmetic and copies ran while one was open for 0% of the time, Pallas kernels for 7%

profile of v2, /device:TPU:11, one launch (start us, length us, event | category | flops | bytes accessed | tf_op | source)
XLA Modules:
  0.0 36.7 jit_solution(17566208477530778555)
XLA Ops:
  0.6 2.7 %first.1 = (f32[32,1024]{1,0:T(8,128)S(1)}, f32[32,1024]{1,0:T(8,128)S(1)}, f32[4,16,128]{2,1,0:T(8,128)S(1)}) custom-call(s32[3]{0:T(128)} %view_h.1, s32[4,169]{1,0:T(4,128)} %bitcast.5, f32[33,2,256]{2,1,0:T(2,128)} %bitcast.3, f32[33,2,256]{2,1,0:T(2,128)} %bitcast.4, f32[4,32,1024]{2,1,0:T(8,128)} %volume.3, f32[3,32,1024]{2,1,0:T(8,128)} %measured.5), custom_call_target="tpu_custom_call" | custom-call | flops 419430400 | bytes 4194304 | tf_op jit(solution)/shard_map/first/pallas_call | solution.py:307
  3.3 0.7 %collective-permute-start = (f32[32,1024]{1,0:T(8,128)S(1)}, f32[32,1024]{1,0:T(8,128)S(1)}, u32[]{:S(2)}, u32[]{:S(2)}) collective-permute-start(f32[32,1024]{1,0:T(8,128)S(1)} %get-tuple-element.42), channel_id=1, source_target_pairs={{0,16},{16,0},{1,17},{17,1},{2,18},{18,2},{3,19},{19,3},{4,20},{20... | collective-permute-start | bytes 393224 | tf_op jit(solution)/shard_map/ppermute | solution.py:338
  4.1 1.0 %collective-permute-done = f32[32,1024]{1,0:T(8,128)S(1)} collective-permute-done((f32[32,1024]{1,0:T(8,128)S(1)}, f32[32,1024]{1,0:T(8,128)S(1)}, u32[]{:S(2)}, u32[]{:S(2)}) %collective-permute-start) | collective-permute-done | bytes 131104 | tf_op jit(solution)/shard_map/ppermute | solution.py:338
  5.1 1.3 %collective-permute-start.1 = (f32[32,1024]{1,0:T(8,128)S(1)}, f32[32,1024]{1,0:T(8,128)S(1)}, u32[]{:S(2)}, u32[]{:S(2)}) collective-permute-start(f32[32,1024]{1,0:T(8,128)S(1)} %add.18.kept), channel_id=1, source_target_pairs={{0,16},{1,0},{2,3},{3,2},{4,5},{5,4},{6,7},{7,6},{8,9},{9,8},{10,1... | collective-permute-start | bytes 393224 | tf_op jit(solution)/shard_map/ppermute | solution.py:339
  6.3 0.0 copy-start.1
  6.3 1.8 %prepare.2 = (bf16[4,256,256]{2,1,0:T(8,128)(2,1)S(1)}, bf16[4,256,256]{2,1,0:T(8,128)(2,1)S(1)}, bf16[64,256]{1,0:T(8,128)(2,1)S(1)}, bf16[64,256]{1,0:T(8,128)...) custom-call(f32[4,16,128]{2,1,0:T(8,128)S(1)} %get-tuple-element.43.taps), custom_call_target="tpu_custom_call" | custom-call | flops 419430400 | bytes 4194304 | tf_op jit(solution)/shard_map/prepare/pallas_call | solution.py:307
  8.2 0.0 copy-start
  8.2 2.2 %collective-permute-done.1.crossed = f32[32,1024]{1,0:T(8,128)S(1)} collective-permute-done((f32[32,1024]{1,0:T(8,128)S(1)}, f32[32,1024]{1,0:T(8,128)S(1)}, u32[]{:S(2)}, u32[]{:S(2)}) %collective-permute-start.1) | collective-permute-done | bytes 131104 | tf_op jit(solution)/shard_map/ppermute | solution.py:339
  10.4 1.6 %collective-permute-start.2 = (f32[32,1024]{1,0:T(8,128)S(1)}, f32[32,1024]{1,0:T(8,128)S(1)}, u32[]{:S(2)}, u32[]{:S(2)}) collective-permute-start(f32[32,1024]{1,0:T(8,128)S(1)} %select_add_fusion.2), channel_id=1, source_target_pairs={{0,16},{16,0},{1,17},{17,1},{2,18},{18,2},{3,19},{19,3},{4,20},{20... | collective-permute-start | bytes 393224 | tf_op jit(solution)/shard_map/ppermute | solution.py:346
  12.0 1.0 %collective-permute-done.2.swapped = f32[32,1024]{1,0:T(8,128)S(1)} collective-permute-done((f32[32,1024]{1,0:T(8,128)S(1)}, f32[32,1024]{1,0:T(8,128)S(1)}, u32[]{:S(2)}, u32[]{:S(2)}) %collective-permute-start.2) | collective-permute-done | bytes 131104 | tf_op jit(solution)/shard_map/ppermute | solution.py:346
  12.9 0.0 copy-done.1
  12.9 0.0 copy-done
  12.9 1.8 %middle.2 = (f32[32,1024]{1,0:T(8,128)S(1)}, f32[32,1024]{1,0:T(8,128)S(1)}, f32[4,32,1024]{2,1,0:T(8,128)S(1)}) custom-call(f32[32,1024]{1,0:T(8,128)S(1)} %add.18.kept, f32[32,1024]{1,0:T(8,128)S(1)} %collective-permute-done.1.crossed, f32[32,1024]{1,0:T(8,128)S(1)} %collective-permute-done.2.swapped, bf16[4,2,256,256]{3,2,1,0:T(8,128)(2,1)S(1)} %get-tuple-element.53.adj, ...), custom_call_target="tpu_custom_call" | custom-call | flops 838860800 | bytes 4194304 | tf_op jit(solution)/shard_map/middle/pallas_call | solution.py:307
  14.7 0.4 %collective-permute-start.3 = (f32[32,1024]{1,0:T(8,128)S(1)}, f32[32,1024]{1,0:T(8,128)S(1)}, u32[]{:S(2)}, u32[]{:S(2)}) collective-permute-start(f32[32,1024]{1,0:T(8,128)S(1)} %get-tuple-element.60), channel_id=1, source_target_pairs={{0,16},{16,0},{1,17},{17,1},{2,18},{18,2},{3,19},{19,3},{4,20},{20... | collective-permute-start | bytes 393224 | tf_op jit(solution)/shard_map/ppermute | solution.py:338
  15.2 1.0 %collective-permute-done.3 = f32[32,1024]{1,0:T(8,128)S(1)} collective-permute-done((f32[32,1024]{1,0:T(8,128)S(1)}, f32[32,1024]{1,0:T(8,128)S(1)}, u32[]{:S(2)}, u32[]{:S(2)}) %collective-permute-start.3) | collective-permute-done | bytes 131104 | tf_op jit(solution)/shard_map/ppermute | solution.py:338
  16.2 1.3 %collective-permute-start.4 = (f32[32,1024]{1,0:T(8,128)S(1)}, f32[32,1024]{1,0:T(8,128)S(1)}, u32[]{:S(2)}, u32[]{:S(2)}) collective-permute-start(f32[32,1024]{1,0:T(8,128)S(1)} %add.20.kept), channel_id=1, source_target_pairs={{0,16},{1,0},{2,3},{3,2},{4,5},{5,4},{6,7},{7,6},{8,9},{9,8},{10,1... | collective-permute-start | bytes 393224 | tf_op jit(solution)/shard_map/ppermute | solution.py:339
  17.4 0.8 %prepare.3 = (bf16[4,256,256]{2,1,0:T(8,128)(2,1)S(1)}, bf16[4,256,256]{2,1,0:T(8,128)(2,1)S(1)}, bf16[64,256]{1,0:T(8,128)(2,1)S(1)}, bf16[64,256]{1,0:T(8,128)...) custom-call(f32[4,16,128]{2,1,0:T(8,128)S(1)} %get-tuple-element.43.taps), custom_call_target="tpu_custom_call" | custom-call | flops 419430400 | bytes 4194304 | tf_op jit(solution)/shard_map/prepare/pallas_call | solution.py:307
  18.2 4.1 %collective-permute-done.4.crossed = f32[32,1024]{1,0:T(8,128)S(1)} collective-permute-done((f32[32,1024]{1,0:T(8,128)S(1)}, f32[32,1024]{1,0:T(8,128)S(1)}, u32[]{:S(2)}, u32[]{:S(2)}) %collective-permute-start.4) | collective-permute-done | bytes 131104 | tf_op jit(solution)/shard_map/ppermute | solution.py:339
  22.3 0.7 %collective-permute-start.5 = (f32[32,1024]{1,0:T(8,128)S(1)}, f32[32,1024]{1,0:T(8,128)S(1)}, u32[]{:S(2)}, u32[]{:S(2)}) collective-permute-start(f32[32,1024]{1,0:T(8,128)S(1)} %select_add_fusion.1), channel_id=1, source_target_pairs={{0,16},{16,0},{1,17},{17,1},{2,18},{18,2},{3,19},{19,3},{4,20},{20... | collective-permute-start | bytes 393224 | tf_op jit(solution)/shard_map/ppermute | solution.py:346
  23.0 1.0 %collective-permute-done.5.swapped = f32[32,1024]{1,0:T(8,128)S(1)} collective-permute-done((f32[32,1024]{1,0:T(8,128)S(1)}, f32[32,1024]{1,0:T(8,128)S(1)}, u32[]{:S(2)}, u32[]{:S(2)}) %collective-permute-start.5) | collective-permute-done | bytes 131104 | tf_op jit(solution)/shard_map/ppermute | solution.py:346
  24.0 1.8 %middle.3 = (f32[32,1024]{1,0:T(8,128)S(1)}, f32[32,1024]{1,0:T(8,128)S(1)}, f32[4,32,1024]{2,1,0:T(8,128)S(1)}) custom-call(f32[32,1024]{1,0:T(8,128)S(1)} %add.20.kept, f32[32,1024]{1,0:T(8,128)S(1)} %collective-permute-done.4.crossed, f32[32,1024]{1,0:T(8,128)S(1)} %collective-permute-done.5.swapped, bf16[4,2,256,256]{3,2,1,0:T(8,128)(2,1)S(1)} %get-tuple-element.68.adj, ...), custom_call_target="tpu_custom_call" | custom-call | flops 838860800 | bytes 4194304 | tf_op jit(solution)/shard_map/middle/pallas_call | solution.py:307
  25.8 0.4 %collective-permute-start.6 = (f32[32,1024]{1,0:T(8,128)S(1)}, f32[32,1024]{1,0:T(8,128)S(1)}, u32[]{:S(2)}, u32[]{:S(2)}) collective-permute-start(f32[32,1024]{1,0:T(8,128)S(1)} %get-tuple-element.76), channel_id=1, source_target_pairs={{0,16},{16,0},{1,17},{17,1},{2,18},{18,2},{3,19},{19,3},{4,20},{20... | collective-permute-start | bytes 393224 | tf_op jit(solution)/shard_map/ppermute | solution.py:338
  26.2 1.0 %collective-permute-done.6 = f32[32,1024]{1,0:T(8,128)S(1)} collective-permute-done((f32[32,1024]{1,0:T(8,128)S(1)}, f32[32,1024]{1,0:T(8,128)S(1)}, u32[]{:S(2)}, u32[]{:S(2)}) %collective-permute-start.6) | collective-permute-done | bytes 131104 | tf_op jit(solution)/shard_map/ppermute | solution.py:338
  27.2 1.1 %collective-permute-start.7 = (f32[32,1024]{1,0:T(8,128)S(1)}, f32[32,1024]{1,0:T(8,128)S(1)}, u32[]{:S(2)}, u32[]{:S(2)}) collective-permute-start(f32[32,1024]{1,0:T(8,128)S(1)} %add.22.kept), channel_id=1, source_target_pairs={{0,16},{1,0},{2,3},{3,2},{4,5},{5,4},{6,7},{7,6},{8,9},{9,8},{10,1... | collective-permute-start | bytes 393224 | tf_op jit(solution)/shard_map/ppermute | solution.py:339
  28.4 5.0 %collective-permute-done.7.crossed = f32[32,1024]{1,0:T(8,128)S(1)} collective-permute-done((f32[32,1024]{1,0:T(8,128)S(1)}, f32[32,1024]{1,0:T(8,128)S(1)}, u32[]{:S(2)}, u32[]{:S(2)}) %collective-permute-start.7) | collective-permute-done | bytes 131104 | tf_op jit(solution)/shard_map/ppermute | solution.py:339
  33.4 0.7 %collective-permute-start.8 = (f32[32,1024]{1,0:T(8,128)S(1)}, f32[32,1024]{1,0:T(8,128)S(1)}, u32[]{:S(2)}, u32[]{:S(2)}) collective-permute-start(f32[32,1024]{1,0:T(8,128)S(1)} %select_add_fusion), channel_id=1, source_target_pairs={{0,16},{16,0},{1,17},{17,1},{2,18},{18,2},{3,19},{19,3},{4,20},{20... | collective-permute-start | bytes 393224 | tf_op jit(solution)/shard_map/ppermute | solution.py:346
  34.1 1.0 %collective-permute-done.8.swapped = f32[32,1024]{1,0:T(8,128)S(1)} collective-permute-done((f32[32,1024]{1,0:T(8,128)S(1)}, f32[32,1024]{1,0:T(8,128)S(1)}, u32[]{:S(2)}, u32[]{:S(2)}) %collective-permute-start.8) | collective-permute-done | bytes 131104 | tf_op jit(solution)/shard_map/ppermute | solution.py:346
  35.1 1.7 %last.1 = (f32[4,32,1024]{2,1,0:T(8,128)}, f32[32,1024]{1,0:T(8,128)}) custom-call(f32[32,1024]{1,0:T(8,128)S(1)} %add.22.kept, f32[32,1024]{1,0:T(8,128)S(1)} %collective-permute-done.7.crossed, f32[32,1024]{1,0:T(8,128)S(1)} %collective-permute-done.8.swapped, bf16[4,2,256,256]{3,2,1,0:T(8,128)(2,1)S(1)} %get-tuple-element.77.adj, ...), custom_call_target="tpu_custom_call" | custom-call | flops 419430400 | bytes 4194304 | tf_op jit(solution)/shard_map/last/pallas_call | solution.py:307
  (6 shorter events, 0.1 us)
Async XLA Ops:
  3.3 1.7 %collective-permute-start = (f32[32,1024]{1,0:T(8,128)S(1)}, f32[32,1024]{1,0:T(8,128)S(1)}, u32[]{:S(2)}, u32[]{:S(2)}) collective-permute-start(f32[32,1024]{1,0:T(8,128)S(1)} %get-tuple-element.42), channel_id=1, source_target_pairs={{0,16},{16,0},{1,17},{17,1},{2,18},{18,2},{3,19},{19,3},{4,20},{20... | collective-permute-start | bytes 393224 | tf_op jit(solution)/shard_map/ppermute | solution.py:338
  5.1 5.3 %collective-permute-start.1 = (f32[32,1024]{1,0:T(8,128)S(1)}, f32[32,1024]{1,0:T(8,128)S(1)}, u32[]{:S(2)}, u32[]{:S(2)}) collective-permute-start(f32[32,1024]{1,0:T(8,128)S(1)} %add.18.kept), channel_id=1, source_target_pairs={{0,16},{1,0},{2,3},{3,2},{4,5},{5,4},{6,7},{7,6},{8,9},{9,8},{10,1... | collective-permute-start | bytes 393224 | tf_op jit(solution)/shard_map/ppermute | solution.py:339
  6.3 6.6 %copy-start.1 = (f32[4,32,1024]{2,1,0:T(8,128)S(1)}, f32[4,32,1024]{2,1,0:T(8,128)}, u32[]{:S(2)}) copy-start(f32[4,32,1024]{2,1,0:T(8,128)} %volume.3) | copy-start | bytes 1572868
  8.2 4.8 %copy-start = (f32[3,32,1024]{2,1,0:T(8,128)S(1)}, f32[3,32,1024]{2,1,0:T(8,128)}, u32[]{:S(2)}) copy-start(f32[3,32,1024]{2,1,0:T(8,128)} %measured.5) | copy-start | bytes 1179652
  10.4 2.5 %collective-permute-start.2 = (f32[32,1024]{1,0:T(8,128)S(1)}, f32[32,1024]{1,0:T(8,128)S(1)}, u32[]{:S(2)}, u32[]{:S(2)}) collective-permute-start(f32[32,1024]{1,0:T(8,128)S(1)} %select_add_fusion.2), channel_id=1, source_target_pairs={{0,16},{16,0},{1,17},{17,1},{2,18},{18,2},{3,19},{19,3},{4,20},{20... | collective-permute-start | bytes 393224 | tf_op jit(solution)/shard_map/ppermute | solution.py:346
  14.7 1.4 %collective-permute-start.3 = (f32[32,1024]{1,0:T(8,128)S(1)}, f32[32,1024]{1,0:T(8,128)S(1)}, u32[]{:S(2)}, u32[]{:S(2)}) collective-permute-start(f32[32,1024]{1,0:T(8,128)S(1)} %get-tuple-element.60), channel_id=1, source_target_pairs={{0,16},{16,0},{1,17},{17,1},{2,18},{18,2},{3,19},{19,3},{4,20},{20... | collective-permute-start | bytes 393224 | tf_op jit(solution)/shard_map/ppermute | solution.py:338
  16.2 6.2 %collective-permute-start.4 = (f32[32,1024]{1,0:T(8,128)S(1)}, f32[32,1024]{1,0:T(8,128)S(1)}, u32[]{:S(2)}, u32[]{:S(2)}) collective-permute-start(f32[32,1024]{1,0:T(8,128)S(1)} %add.20.kept), channel_id=1, source_target_pairs={{0,16},{1,0},{2,3},{3,2},{4,5},{5,4},{6,7},{7,6},{8,9},{9,8},{10,1... | collective-permute-start | bytes 393224 | tf_op jit(solution)/shard_map/ppermute | solution.py:339
  22.3 1.7 %collective-permute-start.5 = (f32[32,1024]{1,0:T(8,128)S(1)}, f32[32,1024]{1,0:T(8,128)S(1)}, u32[]{:S(2)}, u32[]{:S(2)}) collective-permute-start(f32[32,1024]{1,0:T(8,128)S(1)} %select_add_fusion.1), channel_id=1, source_target_pairs={{0,16},{16,0},{1,17},{17,1},{2,18},{18,2},{3,19},{19,3},{4,20},{20... | collective-permute-start | bytes 393224 | tf_op jit(solution)/shard_map/ppermute | solution.py:346
  25.8 1.4 %collective-permute-start.6 = (f32[32,1024]{1,0:T(8,128)S(1)}, f32[32,1024]{1,0:T(8,128)S(1)}, u32[]{:S(2)}, u32[]{:S(2)}) collective-permute-start(f32[32,1024]{1,0:T(8,128)S(1)} %get-tuple-element.76), channel_id=1, source_target_pairs={{0,16},{16,0},{1,17},{17,1},{2,18},{18,2},{3,19},{19,3},{4,20},{20... | collective-permute-start | bytes 393224 | tf_op jit(solution)/shard_map/ppermute | solution.py:338
  27.2 6.2 %collective-permute-start.7 = (f32[32,1024]{1,0:T(8,128)S(1)}, f32[32,1024]{1,0:T(8,128)S(1)}, u32[]{:S(2)}, u32[]{:S(2)}) collective-permute-start(f32[32,1024]{1,0:T(8,128)S(1)} %add.22.kept), channel_id=1, source_target_pairs={{0,16},{1,0},{2,3},{3,2},{4,5},{5,4},{6,7},{7,6},{8,9},{9,8},{10,1... | collective-permute-start | bytes 393224 | tf_op jit(solution)/shard_map/ppermute | solution.py:339
  33.4 1.7 %collective-permute-start.8 = (f32[32,1024]{1,0:T(8,128)S(1)}, f32[32,1024]{1,0:T(8,128)S(1)}, u32[]{:S(2)}, u32[]{:S(2)}) collective-permute-start(f32[32,1024]{1,0:T(8,128)S(1)} %select_add_fusion), channel_id=1, source_target_pairs={{0,16},{16,0},{1,17},{17,1},{2,18},{18,2},{3,19},{19,3},{4,20},{20... | collective-permute-start | bytes 393224 | tf_op jit(solution)/shard_map/ppermute | solution.py:346

commit v3 on v2

--- a/solution.py
+++ b/solution.py
@@ -136,7 +136,7 @@
     return jnp.concatenate([hi, hi, lo], axis=1)
 
 
-def forward(volume, fwd_hi, fwd_lo, row_hi, row_lo, target, w_hi, w_lo):
+def forward(volume, fwd_hi, fwd_lo, row_hi, row_lo, w_hi, w_lo):
     planes = len(volume)
     rows, width = volume[0].shape
     blocks = width // LANES
@@ -160,8 +160,11 @@
                 hi_w, lo_w = split(block)
                 w_hi[spot, c * LANES : (c + 1) * LANES] = hi_w
                 w_lo[spot, c * LANES : (c + 1) * LANES] = lo_w
-    image = dot(row_hi, w_hi[...]) + dot(row_lo, w_hi[...]) + dot(row_hi, w_lo[...])
-    return image[:rows] - target, image[rows:]
+    return row_pass(row_hi[rows:], row_lo[rows:], w_hi, w_lo)
+
+
+def row_pass(row_hi, row_lo, w_hi, w_lo):
+    return dot(row_hi, w_hi[...]) + dot(row_lo, w_hi[...]) + dot(row_hi, w_lo[...])
 
 
 def adjoint(residual, adj_rows, adj, volume, emit):
@@ -172,7 +175,8 @@
     upper = dot(adj_rows, jnp.concatenate([hi, lo, hi], axis=0))
     left = lane_iota((rows, LANES)) < HALF
     result = []
-    for d in range(planes):
+
+    def product(d):
         total = None
         for r in range(2):
             spot = (2 * d + r) * rows
@@ -185,6 +189,11 @@
                 side = jnp.concatenate([side[:-rows], side[rows:]], axis=1)
                 term = dot(side, adj[d, r])
                 total = term if total is None else total + term
+        return total
+
+    ahead = product(0)
+    for d in range(planes):
+        total, ahead = ahead, product(d + 1) if d + 1 < planes else None
         grad = total[:, :LANES] + total[:, LANES:]
         grad = jnp.concatenate([grad[c * rows : (c + 1) * rows] for c in range(blocks)], axis=1)
         moved = volume[d] - descent_step * grad
@@ -210,12 +219,13 @@
 
 
 def first_kernel(
-    paired, view_h, index, row_bank, col_bank, volume, measured, mine, other, taps,
-    view, index_v, row_v, col_v, volume_v, measured_v, fwd_hi, fwd_lo, w_hi, w_lo, sems,
+    paired, view_h, index, row_bank, col_bank, volume, measured,
+    other, taps, measured_v, row_hi, row_lo, w_hi, w_lo,
+    view, index_v, row_v, col_v, volume_v, fwd_hi, fwd_lo, sems,
 ):
     pairs = [(view_h, view), (index, index_v)]
     pairs += [(b.at[:, r, :], v.at[r]) for b, v in ((col_bank, col_v), (row_bank, row_v)) for r in range(2)]
-    pairs += [(volume, volume_v), (measured.at[0], measured_v)]
+    pairs += [(volume, volume_v), (measured.at[0], measured_v.at[0])]
     copies = [pltpu.make_async_copy(a, b, sems.at[i]) for i, (a, b) in enumerate(pairs)]
     for copy in copies:
         copy.start()
@@ -227,13 +237,21 @@
     pick_taps(view.shape[0], planes, view, index_v[...], (row_v, col_v), taps)
     for d in range(planes):
         column_operands(taps, d, d, reach, (fwd_hi, fwd_lo), None)
-    row_hi, row_lo = split(row_operand(taps, 0, planes, reach, place))
+    hi, lo = split(row_operand(taps, 0, planes, reach, place))
+    row_hi[...], row_lo[...] = hi, lo
     for copy in copies[6:]:
         copy.wait()
-    target = window_target(measured_v[...], place) if paired else 0.0
-    mine[...], other[...] = forward(
-        [volume_v[d] for d in range(planes)], fwd_hi, fwd_lo, row_hi, row_lo, target, w_hi, w_lo
-    )
+    other[...] = forward(
+        [volume_v[d] for d in range(planes)], fwd_hi, fwd_lo, hi, lo, w_hi, w_lo
+    )
+
+
+def keep_kernel(paired, step, measured, row_hi, row_lo, w_hi, w_lo, mine):
+    rows = mine.shape[0]
+    image = row_pass(row_hi[:rows], row_lo[:rows], w_hi, w_lo)
+    if paired:
+        image = image - window_target(measured[step], Place(paired))
+    mine[...] = image
 
 
 def prepare_kernel(paired, planes, reach, back, ahead, taps, *outs):
@@ -254,8 +272,8 @@
 
 
 def middle_kernel(
-    paired, step, kept, crossed, swapped, adj, adj_rows, fwd_hi, fwd_lo, row_hi, row_lo,
-    volume, measured, mine, other, fresh, w_hi, w_lo,
+    paired, kept, crossed, swapped, adj, adj_rows, fwd_hi, fwd_lo, row_hi, row_lo, volume,
+    other, fresh, w_hi, w_lo,
 ):
     place = Place(paired)
     residual = jnp.concatenate(joined(place, kept[...], crossed[...], swapped[...]), axis=0)
@@ -265,10 +283,7 @@
 
     planes = [volume[d] for d in range(volume.shape[0])]
     planes = adjoint(residual, adj_rows[...], adj, planes, emit)
-    target = window_target(measured[step], place) if paired else 0.0
-    mine[...], other[...] = forward(
-        planes, fwd_hi, fwd_lo, row_hi[...], row_lo[...], target, w_hi, w_lo
-    )
+    other[...] = forward(planes, fwd_hi, fwd_lo, row_hi[...], row_lo[...], w_hi, w_lo)
 
 
 def last_kernel(
@@ -332,10 +347,10 @@
             return i ^ 1 if side else tiles + i
         return tiles + (i + 1 if i % 2 else i - 1) if side else i ^ 1
 
-    def exchange(mine, other, step, during):
+    def exchange(keep, other, step, during):
         if paired:
             swap = [(0, 1), (1, 0)]
-            kept = mine + lax.ppermute(other, "depth", swap)
+            kept = sum(lax.optimization_barrier((keep(), lax.ppermute(other, "depth", swap))))
             crossed = lax.ppermute(
                 kept, ("depth", "tile"), [(i, flow(i)) for i in range(2 * tiles)]
             )
@@ -351,7 +366,7 @@
         evens = [(i, i ^ 1) for i in range(tiles) if i ^ 1 < tiles]
         odds = [(i, i + 1 if i % 2 else i - 1) for i in range(tiles)]
         odds = [(i, j) for i, j in odds if 0 <= j < tiles]
-        kept = lax.psum(mine, "depth") - jnp.where(lower, low, high)
+        kept = lax.psum(keep(), "depth") - jnp.where(lower, low, high)
         rest = lax.psum(other, "depth") - jnp.where(lower, high, low)
         rest = rest + lax.ppermute(rest, "tile", odds)
         return kept, lax.ppermute(kept, "tile", evens), rest, during()
@@ -372,24 +387,31 @@
     block = shape(volume.shape, f32)
     lines = -(-steps * planes // 16) * 16
     tap_shape = shape((4, lines, LANES), f32)
-    scratch = [pltpu.VMEM((stacks, width), bf16)] * 2
+    columns = [shape((stacks, width), bf16)] * 2
     work = 400 << 20
 
     index = kernel_index.T
     banks = [jnp.transpose(x, (2, 1, 0)) for x in (row_bank, col_bank)]
-    mine, other, taps = call(
-        functools.partial(first_kernel, paired), [HBM] * 6, [VMEM] * 3,
-        [image, image, tap_shape],
+    outs = [image, tap_shape, shape((1, rows, width), f32), *forward_shapes[2:], *columns]
+    other, taps, target, row_hi, row_lo, *wide = call(
+        functools.partial(first_kernel, paired), [HBM] * 6, [VMEM] * len(outs), outs,
         [pltpu.SMEM(view_order.shape, jnp.int32)]
         + [pltpu.VMEM(index.shape, index.dtype)]
         + [pltpu.VMEM((2, x.shape[0], x.shape[2]), f32) for x in banks]
-        + [pltpu.VMEM(x.shape, f32) for x in (volume, measured[0])]
-        + [pltpu.VMEM(x.shape, x.dtype) for x in forward_shapes[:2]]
-        + scratch + [pltpu.SemaphoreType.DMA((8,))],
+        + [pltpu.VMEM(x.shape, x.dtype) for x in (volume, *forward_shapes[:2])]
+        + [pltpu.SemaphoreType.DMA((8,))],
         work, "first",
         [pltpu.with_memory_space_constraint(x, pltpu.HBM)
          for x in (view_order, index, *banks, volume, measured)],
     )
+
+    def keeper(step, *args):
+        return lambda: call(
+            functools.partial(keep_kernel, paired, step), [VMEM] * 5, [VMEM], [image], [],
+            work // 10, "keep", args,
+        )[0]
+
+    keep = keeper(0, target, row_hi, row_lo, *wide)
 
     def prepare(back, ahead):
         outs = forward_shapes + adjoint_shapes * len(back)
@@ -402,16 +424,18 @@
     for step in range(1, steps):
         back = (0, 1) if step == 1 else (step,)
         kept, crossed, swapped, ready = exchange(
-            mine, other, step - 1, lambda: prepare(back, step)
+            keep, other, step - 1, lambda: prepare(back, step)
         )
         forwards = ready[:4]
         adjoints += [ready[i : i + 2] for i in range(4, len(ready), 2)]
-        mine, other, volume = call(
-            functools.partial(middle_kernel, paired, step), [VMEM] * 11, [VMEM] * 3,
-            [image, image, block], scratch, 2 * work, "middle",
-            (kept, crossed, swapped, *adjoints[step - 1], *forwards, volume, measured),
-        )
-    kept, crossed, swapped, _ = exchange(mine, other, steps - 1, lambda: [])
+        outs = [image, block, *columns]
+        other, volume, *wide = call(
+            functools.partial(middle_kernel, paired), [VMEM] * 10, [VMEM] * 4, outs, [],
+            2 * work, "middle",
+            (kept, crossed, swapped, *adjoints[step - 1], *forwards, volume),
+        )
+        keep = keeper(step, measured, *forwards[2:], *wide)
+    kept, crossed, swapped, _ = exchange(keep, other, steps - 1, lambda: [])
     return call(
         functools.partial(last_kernel, paired), [VMEM] * 6, [HBM] * 2, [block, image],
         [pltpu.VMEM(volume.shape, f32), pltpu.VMEM((rows, width), f32),

time: 36.9 us -> 36.8 us (level)
  Pallas kernels: 10.5 us -> 11.5 us
  waiting for transfers between devices: 17.2 us -> 16.2 us
    ppermute x3, waiting for transfers between devices: 2.96 us -> 1.86 us  [exchange(): lax.ppermute(other, 'depth', swap)]
    pallas_call x6 -> x9, Pallas kernels: 10.5 us -> 11.5 us  [call(): pl.pallas_call(kernel, out_shape=outs, in_specs=in_specs, out_specs=out_s...]
  transfers between devices with their start and end apart: 9 -> 9, of which waited for: 9 -> 9; matrix products, arithmetic and copies ran while one was open for 0% -> 0% of each run, Pallas kernels for 7% -> 10%
where the time goes in v3:
time: 36.8 us; the launch traced here: 36.6 us
  waiting for transfers between devices  16.2 us (44%)
  Pallas kernels  11.5 us (31%)
  starting transfers between devices  8.15 us (22%)
  between operations  0.7 us (2%)
    pallas_call x9, Pallas kernels, call(): pl.pallas_call(kernel, out_shape=outs, in_specs=in_specs, out_specs=out_s...  11.5 us
    ppermute x3, waiting for transfers between devices, exchange(): lax.ppermute(kept, ('depth', 'tile'), [(i, flow(i)) for i in range(2 * ti...  11.3 us
    ppermute x3, starting transfers between devices, exchange(): lax.ppermute(kept, ('depth', 'tile'), [(i, flow(i)) for i in range(2 * ti...  3.66 us
    ppermute x3, waiting for transfers between devices, exchange(): return (kept, crossed, lax.ppermute(send, 'depth', swap), ready)  2.96 us
    ppermute x3, starting transfers between devices, exchange(): return (kept, crossed, lax.ppermute(send, 'depth', swap), ready)  2.93 us
    ppermute x3, waiting for transfers between devices, exchange(): lax.ppermute(other, 'depth', swap)  1.86 us
    ppermute x3, starting transfers between devices, exchange(): lax.ppermute(other, 'depth', swap)  1.56 us
  transfers between devices with their start and end apart: 9, of which 9 were waited for; matrix products, arithmetic and copies ran while one was open for 0% of the time, Pallas kernels for 10%

profile of v3, /device:TPU:11, one launch (start us, length us, event | category | flops | bytes accessed | tf_op | source)
XLA Modules:
  0.0 36.6 jit_solution(16898339590114354637)
XLA Ops:
  0.6 2.7 %first.1 = (f32[32,1024]{1,0:T(8,128)S(1)}, f32[4,16,128]{2,1,0:T(8,128)S(1)}, f32[1,32,1024]{2,1,0:T(8,128)S(1)}, bf16[64,256]{1,0:T(8,128)(2,1)S(1)}, bf16[64,...) custom-call(s32[3]{0:T(128)} %view_h.1, s32[4,169]{1,0:T(4,128)} %bitcast.5, ...), custom_call_target="tpu_custom_call" | custom-call | flops 419430400 | bytes 4194304 | tf_op jit(solution)/shard_map/first/pallas_call | solution.py:322
  3.3 0.7 %collective-permute-start = (f32[32,1024]{1,0:T(8,128)S(1)}, f32[32,1024]{1,0:T(8,128)S(1)}, u32[]{:S(2)}, u32[]{:S(2)}) collective-permute-start(f32[32,1024]{1,0:T(8,128)S(1)} %get-tuple-element.58), channel_id=1, source_target_pairs={{0,16},{16,0},{1,17},{17,1},{2,18},{18,2},{3,19},{19,3},{4,20},{20... | collective-permute-start | bytes 393224 | tf_op jit(solution)/shard_map/ppermute | solution.py:353
  4.1 0.4 keep.3
  4.4 0.6 %collective-permute-done = f32[32,1024]{1,0:T(8,128)S(1)} collective-permute-done((f32[32,1024]{1,0:T(8,128)S(1)}, f32[32,1024]{1,0:T(8,128)S(1)}, u32[]{:S(2)}, u32[]{:S(2)}) %collective-permute-start) | collective-permute-done | bytes 131104 | tf_op jit(solution)/shard_map/ppermute | solution.py:353
  5.1 1.3 %collective-permute-start.1 = (f32[32,1024]{1,0:T(8,128)S(1)}, f32[32,1024]{1,0:T(8,128)S(1)}, u32[]{:S(2)}, u32[]{:S(2)}) collective-permute-start(f32[32,1024]{1,0:T(8,128)S(1)} %add.18.kept), channel_id=1, source_target_pairs={{0,16},{1,0},{2,3},{3,2},{4,5},{5,4},{6,7},{7,6},{8,9},{9,8},{10,1... | collective-permute-start | bytes 393224 | tf_op jit(solution)/shard_map/ppermute | solution.py:354
  6.3 0.0 copy-start.1
  6.3 1.8 %prepare.2 = (bf16[4,256,256]{2,1,0:T(8,128)(2,1)S(1)}, bf16[4,256,256]{2,1,0:T(8,128)(2,1)S(1)}, bf16[64,256]{1,0:T(8,128)(2,1)S(1)}, bf16[64,256]{1,0:T(8,128)...) custom-call(f32[4,16,128]{2,1,0:T(8,128)S(1)} %get-tuple-element.61.taps), custom_call_target="tpu_custom_call" | custom-call | flops 419430400 | bytes 4194304 | tf_op jit(solution)/shard_map/prepare/pallas_call | solution.py:322
  8.1 2.2 %collective-permute-done.1.crossed = f32[32,1024]{1,0:T(8,128)S(1)} collective-permute-done((f32[32,1024]{1,0:T(8,128)S(1)}, f32[32,1024]{1,0:T(8,128)S(1)}, u32[]{:S(2)}, u32[]{:S(2)}) %collective-permute-start.1) | collective-permute-done | bytes 131104 | tf_op jit(solution)/shard_map/ppermute | solution.py:354
  10.4 0.0 copy-start
  10.4 1.6 %collective-permute-start.2 = (f32[32,1024]{1,0:T(8,128)S(1)}, f32[32,1024]{1,0:T(8,128)S(1)}, u32[]{:S(2)}, u32[]{:S(2)}) collective-permute-start(f32[32,1024]{1,0:T(8,128)S(1)} %select_add_fusion.2), channel_id=1, source_target_pairs={{0,16},{16,0},{1,17},{17,1},{2,18},{18,2},{3,19},{19,3},{4,20},{20... | collective-permute-start | bytes 393224 | tf_op jit(solution)/shard_map/ppermute | solution.py:361
  11.9 1.0 %collective-permute-done.2.swapped = f32[32,1024]{1,0:T(8,128)S(1)} collective-permute-done((f32[32,1024]{1,0:T(8,128)S(1)}, f32[32,1024]{1,0:T(8,128)S(1)}, u32[]{:S(2)}, u32[]{:S(2)}) %collective-permute-start.2) | collective-permute-done | bytes 131104 | tf_op jit(solution)/shard_map/ppermute | solution.py:361
  12.9 0.0 copy-done.1
  12.9 1.7 %middle.2 = (f32[32,1024]{1,0:T(8,128)S(1)}, f32[4,32,1024]{2,1,0:T(8,128)S(1)}, bf16[256,1024]{1,0:T(8,128)(2,1)S(1)}, bf16[256,1024]{1,0:T(8,128)(2,1)S(1)}) custom-call(f32[32,1024]{1,0:T(8,128)S(1)} %add.18.kept, f32[32,1024]{1,0:T(8,128)S(1)} %collective-permute-done.1.crossed, f32[32,1024]{1,0:T(8,128)S(1)} %collective-permute-done.2.swapped, ...), custom_call_target="tpu_custom_call" | custom-call | flops 838860800 | bytes 4194304 | tf_op jit(solution)/shard_map/middle/pallas_call | solution.py:322
  14.7 0.4 %collective-permute-start.3 = (f32[32,1024]{1,0:T(8,128)S(1)}, f32[32,1024]{1,0:T(8,128)S(1)}, u32[]{:S(2)}, u32[]{:S(2)}) collective-permute-start(f32[32,1024]{1,0:T(8,128)S(1)} %get-tuple-element.79), channel_id=1, source_target_pairs={{0,16},{16,0},{1,17},{17,1},{2,18},{18,2},{3,19},{19,3},{4,20},{20... | collective-permute-start | bytes 393224 | tf_op jit(solution)/shard_map/ppermute | solution.py:353
  15.1 0.0 copy-done
  15.1 0.4 %keep.4 = f32[32,1024]{1,0:T(8,128)S(1)} custom-call(f32[3,32,1024]{2,1,0:T(8,128)S(1)} %copy-done, bf16[64,256]{1,0:T(8,128)(2,1)S(1)} %get-tuple-element.70.row_hi, bf16[64,256]{1,0:T(8,128)(2,1)S(1)} %get-tuple-element.71.row_lo, bf16[256,1024]{1,0:T(8,128)(2,1)S(1)} %get-tuple-element.77.w_hi, bf16[256,1024]{1,0:T(8,128)(2,1)S(1)} %get-tuple-element.78.w_lo), custom_call_target="tpu_custom_call" | custom-call | flops 41943040 | bytes 4194304 | tf_op jit(solution)/shard_map/keep/pallas_call | solution.py:322
  15.4 0.6 %collective-permute-done.3 = f32[32,1024]{1,0:T(8,128)S(1)} collective-permute-done((f32[32,1024]{1,0:T(8,128)S(1)}, f32[32,1024]{1,0:T(8,128)S(1)}, u32[]{:S(2)}, u32[]{:S(2)}) %collective-permute-start.3) | collective-permute-done | bytes 131104 | tf_op jit(solution)/shard_map/ppermute | solution.py:353
  16.1 1.3 %collective-permute-start.4 = (f32[32,1024]{1,0:T(8,128)S(1)}, f32[32,1024]{1,0:T(8,128)S(1)}, u32[]{:S(2)}, u32[]{:S(2)}) collective-permute-start(f32[32,1024]{1,0:T(8,128)S(1)} %add.20.kept), channel_id=1, source_target_pairs={{0,16},{1,0},{2,3},{3,2},{4,5},{5,4},{6,7},{7,6},{8,9},{9,8},{10,1... | collective-permute-start | bytes 393224 | tf_op jit(solution)/shard_map/ppermute | solution.py:354
  17.3 0.8 %prepare.3 = (bf16[4,256,256]{2,1,0:T(8,128)(2,1)S(1)}, bf16[4,256,256]{2,1,0:T(8,128)(2,1)S(1)}, bf16[64,256]{1,0:T(8,128)(2,1)S(1)}, bf16[64,256]{1,0:T(8,128)...) custom-call(f32[4,16,128]{2,1,0:T(8,128)S(1)} %get-tuple-element.61.taps), custom_call_target="tpu_custom_call" | custom-call | flops 419430400 | bytes 4194304 | tf_op jit(solution)/shard_map/prepare/pallas_call | solution.py:322
  18.1 4.1 %collective-permute-done.4.crossed = f32[32,1024]{1,0:T(8,128)S(1)} collective-permute-done((f32[32,1024]{1,0:T(8,128)S(1)}, f32[32,1024]{1,0:T(8,128)S(1)}, u32[]{:S(2)}, u32[]{:S(2)}) %collective-permute-start.4) | collective-permute-done | bytes 131104 | tf_op jit(solution)/shard_map/ppermute | solution.py:354
  22.3 0.7 %collective-permute-start.5 = (f32[32,1024]{1,0:T(8,128)S(1)}, f32[32,1024]{1,0:T(8,128)S(1)}, u32[]{:S(2)}, u32[]{:S(2)}) collective-permute-start(f32[32,1024]{1,0:T(8,128)S(1)} %select_add_fusion.1), channel_id=1, source_target_pairs={{0,16},{16,0},{1,17},{17,1},{2,18},{18,2},{3,19},{19,3},{4,20},{20... | collective-permute-start | bytes 393224 | tf_op jit(solution)/shard_map/ppermute | solution.py:361
  23.0 1.0 %collective-permute-done.5.swapped = f32[32,1024]{1,0:T(8,128)S(1)} collective-permute-done((f32[32,1024]{1,0:T(8,128)S(1)}, f32[32,1024]{1,0:T(8,128)S(1)}, u32[]{:S(2)}, u32[]{:S(2)}) %collective-permute-start.5) | collective-permute-done | bytes 131104 | tf_op jit(solution)/shard_map/ppermute | solution.py:361
  23.9 1.7 %middle.3 = (f32[32,1024]{1,0:T(8,128)S(1)}, f32[4,32,1024]{2,1,0:T(8,128)S(1)}, bf16[256,1024]{1,0:T(8,128)(2,1)S(1)}, bf16[256,1024]{1,0:T(8,128)(2,1)S(1)}) custom-call(f32[32,1024]{1,0:T(8,128)S(1)} %add.20.kept, f32[32,1024]{1,0:T(8,128)S(1)} %collective-permute-done.4.crossed, f32[32,1024]{1,0:T(8,128)S(1)} %collective-permute-done.5.swapped, ...), custom_call_target="tpu_custom_call" | custom-call | flops 838860800 | bytes 4194304 | tf_op jit(solution)/shard_map/middle/pallas_call | solution.py:322
  25.7 0.4 %collective-permute-start.6 = (f32[32,1024]{1,0:T(8,128)S(1)}, f32[32,1024]{1,0:T(8,128)S(1)}, u32[]{:S(2)}, u32[]{:S(2)}) collective-permute-start(f32[32,1024]{1,0:T(8,128)S(1)} %get-tuple-element.98), channel_id=1, source_target_pairs={{0,16},{16,0},{1,17},{17,1},{2,18},{18,2},{3,19},{19,3},{4,20},{20... | collective-permute-start | bytes 393224 | tf_op jit(solution)/shard_map/ppermute | solution.py:353
  26.1 0.4 keep.5
  26.4 0.6 %collective-permute-done.6 = f32[32,1024]{1,0:T(8,128)S(1)} collective-permute-done((f32[32,1024]{1,0:T(8,128)S(1)}, f32[32,1024]{1,0:T(8,128)S(1)}, u32[]{:S(2)}, u32[]{:S(2)}) %collective-permute-start.6) | collective-permute-done | bytes 131104 | tf_op jit(solution)/shard_map/ppermute | solution.py:353
  27.1 1.1 %collective-permute-start.7 = (f32[32,1024]{1,0:T(8,128)S(1)}, f32[32,1024]{1,0:T(8,128)S(1)}, u32[]{:S(2)}, u32[]{:S(2)}) collective-permute-start(f32[32,1024]{1,0:T(8,128)S(1)} %add.22.kept), channel_id=1, source_target_pairs={{0,16},{1,0},{2,3},{3,2},{4,5},{5,4},{6,7},{7,6},{8,9},{9,8},{10,1... | collective-permute-start | bytes 393224 | tf_op jit(solution)/shard_map/ppermute | solution.py:354
  28.2 5.0 %collective-permute-done.7.crossed = f32[32,1024]{1,0:T(8,128)S(1)} collective-permute-done((f32[32,1024]{1,0:T(8,128)S(1)}, f32[32,1024]{1,0:T(8,128)S(1)}, u32[]{:S(2)}, u32[]{:S(2)}) %collective-permute-start.7) | collective-permute-done | bytes 131104 | tf_op jit(solution)/shard_map/ppermute | solution.py:354
  33.3 0.7 %collective-permute-start.8 = (f32[32,1024]{1,0:T(8,128)S(1)}, f32[32,1024]{1,0:T(8,128)S(1)}, u32[]{:S(2)}, u32[]{:S(2)}) collective-permute-start(f32[32,1024]{1,0:T(8,128)S(1)} %select_add_fusion), channel_id=1, source_target_pairs={{0,16},{16,0},{1,17},{17,1},{2,18},{18,2},{3,19},{19,3},{4,20},{20... | collective-permute-start | bytes 393224 | tf_op jit(solution)/shard_map/ppermute | solution.py:361
  34.0 1.0 %collective-permute-done.8.swapped = f32[32,1024]{1,0:T(8,128)S(1)} collective-permute-done((f32[32,1024]{1,0:T(8,128)S(1)}, f32[32,1024]{1,0:T(8,128)S(1)}, u32[]{:S(2)}, u32[]{:S(2)}) %collective-permute-start.8) | collective-permute-done | bytes 131104 | tf_op jit(solution)/shard_map/ppermute | solution.py:361
  34.9 1.6 %last.1 = (f32[4,32,1024]{2,1,0:T(8,128)}, f32[32,1024]{1,0:T(8,128)}) custom-call(f32[32,1024]{1,0:T(8,128)S(1)} %add.22.kept, f32[32,1024]{1,0:T(8,128)S(1)} %collective-permute-done.7.crossed, f32[32,1024]{1,0:T(8,128)S(1)} %collective-permute-done.8.swapped, bf16[4,2,256,256]{3,2,1,0:T(8,128)(2,1)S(1)} %get-tuple-element.101.adj, ...), custom_call_target="tpu_custom_call" | custom-call | flops 419430400 | bytes 4194304 | tf_op jit(solution)/shard_map/last/pallas_call | solution.py:322
  (6 shorter events, 0.1 us)
Async XLA Ops:
  3.3 1.7 %collective-permute-start = (f32[32,1024]{1,0:T(8,128)S(1)}, f32[32,1024]{1,0:T(8,128)S(1)}, u32[]{:S(2)}, u32[]{:S(2)}) collective-permute-start(f32[32,1024]{1,0:T(8,128)S(1)} %get-tuple-element.58), channel_id=1, source_target_pairs={{0,16},{16,0},{1,17},{17,1},{2,18},{18,2},{3,19},{19,3},{4,20},{20... | collective-permute-start | bytes 393224 | tf_op jit(solution)/shard_map/ppermute | solution.py:353
  5.1 5.3 %collective-permute-start.1 = (f32[32,1024]{1,0:T(8,128)S(1)}, f32[32,1024]{1,0:T(8,128)S(1)}, u32[]{:S(2)}, u32[]{:S(2)}) collective-permute-start(f32[32,1024]{1,0:T(8,128)S(1)} %add.18.kept), channel_id=1, source_target_pairs={{0,16},{1,0},{2,3},{3,2},{4,5},{5,4},{6,7},{7,6},{8,9},{9,8},{10,1... | collective-permute-start | bytes 393224 | tf_op jit(solution)/shard_map/ppermute | solution.py:354
  6.3 6.6 %copy-start.1 = (f32[4,32,1024]{2,1,0:T(8,128)S(1)}, f32[4,32,1024]{2,1,0:T(8,128)}, u32[]{:S(2)}) copy-start(f32[4,32,1024]{2,1,0:T(8,128)} %volume.3) | copy-start | bytes 1572868
  10.4 4.7 %copy-start = (f32[3,32,1024]{2,1,0:T(8,128)S(1)}, f32[3,32,1024]{2,1,0:T(8,128)}, u32[]{:S(2)}) copy-start(f32[3,32,1024]{2,1,0:T(8,128)} %measured.5) | copy-start | bytes 1179652
  10.4 2.5 %collective-permute-start.2 = (f32[32,1024]{1,0:T(8,128)S(1)}, f32[32,1024]{1,0:T(8,128)S(1)}, u32[]{:S(2)}, u32[]{:S(2)}) collective-permute-start(f32[32,1024]{1,0:T(8,128)S(1)} %select_add_fusion.2), channel_id=1, source_target_pairs={{0,16},{16,0},{1,17},{17,1},{2,18},{18,2},{3,19},{19,3},{4,20},{20... | collective-permute-start | bytes 393224 | tf_op jit(solution)/shard_map/ppermute | solution.py:361
  14.7 1.4 %collective-permute-start.3 = (f32[32,1024]{1,0:T(8,128)S(1)}, f32[32,1024]{1,0:T(8,128)S(1)}, u32[]{:S(2)}, u32[]{:S(2)}) collective-permute-start(f32[32,1024]{1,0:T(8,128)S(1)} %get-tuple-element.79), channel_id=1, source_target_pairs={{0,16},{16,0},{1,17},{17,1},{2,18},{18,2},{3,19},{19,3},{4,20},{20... | collective-permute-start | bytes 393224 | tf_op jit(solution)/shard_map/ppermute | solution.py:353
  16.1 6.2 %collective-permute-start.4 = (f32[32,1024]{1,0:T(8,128)S(1)}, f32[32,1024]{1,0:T(8,128)S(1)}, u32[]{:S(2)}, u32[]{:S(2)}) collective-permute-start(f32[32,1024]{1,0:T(8,128)S(1)} %add.20.kept), channel_id=1, source_target_pairs={{0,16},{1,0},{2,3},{3,2},{4,5},{5,4},{6,7},{7,6},{8,9},{9,8},{10,1... | collective-permute-start | bytes 393224 | tf_op jit(solution)/shard_map/ppermute | solution.py:354
  22.3 1.7 %collective-permute-start.5 = (f32[32,1024]{1,0:T(8,128)S(1)}, f32[32,1024]{1,0:T(8,128)S(1)}, u32[]{:S(2)}, u32[]{:S(2)}) collective-permute-start(f32[32,1024]{1,0:T(8,128)S(1)} %select_add_fusion.1), channel_id=1, source_target_pairs={{0,16},{16,0},{1,17},{17,1},{2,18},{18,2},{3,19},{19,3},{4,20},{20... | collective-permute-start | bytes 393224 | tf_op jit(solution)/shard_map/ppermute | solution.py:361
  25.7 1.4 %collective-permute-start.6 = (f32[32,1024]{1,0:T(8,128)S(1)}, f32[32,1024]{1,0:T(8,128)S(1)}, u32[]{:S(2)}, u32[]{:S(2)}) collective-permute-start(f32[32,1024]{1,0:T(8,128)S(1)} %get-tuple-element.98), channel_id=1, source_target_pairs={{0,16},{16,0},{1,17},{17,1},{2,18},{18,2},{3,19},{19,3},{4,20},{20... | collective-permute-start | bytes 393224 | tf_op jit(solution)/shard_map/ppermute | solution.py:353
  27.1 6.2 %collective-permute-start.7 = (f32[32,1024]{1,0:T(8,128)S(1)}, f32[32,1024]{1,0:T(8,128)S(1)}, u32[]{:S(2)}, u32[]{:S(2)}) collective-permute-start(f32[32,1024]{1,0:T(8,128)S(1)} %add.22.kept), channel_id=1, source_target_pairs={{0,16},{1,0},{2,3},{3,2},{4,5},{5,4},{6,7},{7,6},{8,9},{9,8},{10,1... | collective-permute-start | bytes 393224 | tf_op jit(solution)/shard_map/ppermute | solution.py:354
  33.3 1.7 %collective-permute-start.8 = (f32[32,1024]{1,0:T(8,128)S(1)}, f32[32,1024]{1,0:T(8,128)S(1)}, u32[]{:S(2)}, u32[]{:S(2)}) collective-permute-start(f32[32,1024]{1,0:T(8,128)S(1)} %select_add_fusion), channel_id=1, source_target_pairs={{0,16},{16,0},{1,17},{17,1},{2,18},{18,2},{3,19},{19,3},{4,20},{20... | collective-permute-start | bytes 393224 | tf_op jit(solution)/shard_map/ppermute | solution.py:361

commit v4 on v3

--- a/solution.py
+++ b/solution.py
@@ -298,15 +298,16 @@
         [jnp.where(lower, other[reach:], mine[reach:]), jnp.where(lower, mine[:reach], other[:reach])],
         axis=0,
     )
-    residual_v[...] = pltpu.roll(own, own.shape[1] - HALF, 1)
     count = volume.shape[0]
     copies = [pltpu.make_async_copy(fresh_v.at[d], fresh.at[d], sems.at[d]) for d in range(count)]
     copies.append(pltpu.make_async_copy(residual_v, residual_out, sems.at[count]))
-    copies[count].start()
 
     def emit(d, plane):
         fresh_v[d] = plane
         copies[d].start()
+        if d == 0:
+            residual_v[...] = pltpu.roll(own, own.shape[1] - HALF, 1)
+            copies[count].start()
 
     planes = [volume[d] for d in range(count)]
     adjoint(jnp.concatenate([mine, other], axis=0), adj_rows[...], adj, planes, emit)

time: 36.8 us -> 36.8 us (level)
  no operation moved by 1% of the time
where the time goes in v4:
time: 36.8 us; the launch traced here: 36.6 us
  waiting for transfers between devices  16.2 us (44%)
  Pallas kernels  11.5 us (31%)
  starting transfers between devices  8.15 us (22%)
  between operations  0.7 us (2%)
    pallas_call x9, Pallas kernels, call(): pl.pallas_call(kernel, out_shape=outs, in_specs=in_specs, out_specs=out_s...  11.5 us
    ppermute x3, waiting for transfers between devices, exchange(): lax.ppermute(kept, ('depth', 'tile'), [(i, flow(i)) for i in range(2 * ti...  11.3 us
    ppermute x3, starting transfers between devices, exchange(): lax.ppermute(kept, ('depth', 'tile'), [(i, flow(i)) for i in range(2 * ti...  3.66 us
    ppermute x3, waiting for transfers between devices, exchange(): return (kept, crossed, lax.ppermute(send, 'depth', swap), ready)  2.96 us
    ppermute x3, starting transfers between devices, exchange(): return (kept, crossed, lax.ppermute(send, 'depth', swap), ready)  2.93 us
    ppermute x3, waiting for transfers between devices, exchange(): lax.ppermute(other, 'depth', swap)  1.86 us
    ppermute x3, starting transfers between devices, exchange(): lax.ppermute(other, 'depth', swap)  1.56 us
  transfers between devices with their start and end apart: 9, of which 9 were waited for; matrix products, arithmetic and copies ran while one was open for 0% of the time, Pallas kernels for 10%

profile of v4, /device:TPU:11, one launch (start us, length us, event | category | flops | bytes accessed | tf_op | source)
XLA Modules:
  0.0 36.6 jit_solution(5000501346078717298)
XLA Ops:
  0.6 2.7 %first.1 = (f32[32,1024]{1,0:T(8,128)S(1)}, f32[4,16,128]{2,1,0:T(8,128)S(1)}, f32[1,32,1024]{2,1,0:T(8,128)S(1)}, bf16[64,256]{1,0:T(8,128)(2,1)S(1)}, bf16[64,...) custom-call(s32[3]{0:T(128)} %view_h.1, s32[4,169]{1,0:T(4,128)} %bitcast.5, ...), custom_call_target="tpu_custom_call" | custom-call | flops 419430400 | bytes 4194304 | tf_op jit(solution)/shard_map/first/pallas_call | solution.py:323
  3.3 0.7 %collective-permute-start = (f32[32,1024]{1,0:T(8,128)S(1)}, f32[32,1024]{1,0:T(8,128)S(1)}, u32[]{:S(2)}, u32[]{:S(2)}) collective-permute-start(f32[32,1024]{1,0:T(8,128)S(1)} %get-tuple-element.58), channel_id=1, source_target_pairs={{0,16},{16,0},{1,17},{17,1},{2,18},{18,2},{3,19},{19,3},{4,20},{20... | collective-permute-start | bytes 393224 | tf_op jit(solution)/shard_map/ppermute | solution.py:354
  4.1 0.4 keep.3
  4.4 0.6 %collective-permute-done = f32[32,1024]{1,0:T(8,128)S(1)} collective-permute-done((f32[32,1024]{1,0:T(8,128)S(1)}, f32[32,1024]{1,0:T(8,128)S(1)}, u32[]{:S(2)}, u32[]{:S(2)}) %collective-permute-start) | collective-permute-done | bytes 131104 | tf_op jit(solution)/shard_map/ppermute | solution.py:354
  5.1 1.3 %collective-permute-start.1 = (f32[32,1024]{1,0:T(8,128)S(1)}, f32[32,1024]{1,0:T(8,128)S(1)}, u32[]{:S(2)}, u32[]{:S(2)}) collective-permute-start(f32[32,1024]{1,0:T(8,128)S(1)} %add.18.kept), channel_id=1, source_target_pairs={{0,16},{1,0},{2,3},{3,2},{4,5},{5,4},{6,7},{7,6},{8,9},{9,8},{10,1... | collective-permute-start | bytes 393224 | tf_op jit(solution)/shard_map/ppermute | solution.py:355
  6.3 0.0 copy-start.1
  6.3 1.8 %prepare.2 = (bf16[4,256,256]{2,1,0:T(8,128)(2,1)S(1)}, bf16[4,256,256]{2,1,0:T(8,128)(2,1)S(1)}, bf16[64,256]{1,0:T(8,128)(2,1)S(1)}, bf16[64,256]{1,0:T(8,128)...) custom-call(f32[4,16,128]{2,1,0:T(8,128)S(1)} %get-tuple-element.61.taps), custom_call_target="tpu_custom_call" | custom-call | flops 419430400 | bytes 4194304 | tf_op jit(solution)/shard_map/prepare/pallas_call | solution.py:323
  8.1 2.2 %collective-permute-done.1.crossed = f32[32,1024]{1,0:T(8,128)S(1)} collective-permute-done((f32[32,1024]{1,0:T(8,128)S(1)}, f32[32,1024]{1,0:T(8,128)S(1)}, u32[]{:S(2)}, u32[]{:S(2)}) %collective-permute-start.1) | collective-permute-done | bytes 131104 | tf_op jit(solution)/shard_map/ppermute | solution.py:355
  10.4 0.0 copy-start
  10.4 1.6 %collective-permute-start.2 = (f32[32,1024]{1,0:T(8,128)S(1)}, f32[32,1024]{1,0:T(8,128)S(1)}, u32[]{:S(2)}, u32[]{:S(2)}) collective-permute-start(f32[32,1024]{1,0:T(8,128)S(1)} %select_add_fusion.2), channel_id=1, source_target_pairs={{0,16},{16,0},{1,17},{17,1},{2,18},{18,2},{3,19},{19,3},{4,20},{20... | collective-permute-start | bytes 393224 | tf_op jit(solution)/shard_map/ppermute | solution.py:362
  11.9 1.0 %collective-permute-done.2.swapped = f32[32,1024]{1,0:T(8,128)S(1)} collective-permute-done((f32[32,1024]{1,0:T(8,128)S(1)}, f32[32,1024]{1,0:T(8,128)S(1)}, u32[]{:S(2)}, u32[]{:S(2)}) %collective-permute-start.2) | collective-permute-done | bytes 131104 | tf_op jit(solution)/shard_map/ppermute | solution.py:362
  12.9 0.0 copy-done.1
  12.9 1.7 %middle.2 = (f32[32,1024]{1,0:T(8,128)S(1)}, f32[4,32,1024]{2,1,0:T(8,128)S(1)}, bf16[256,1024]{1,0:T(8,128)(2,1)S(1)}, bf16[256,1024]{1,0:T(8,128)(2,1)S(1)}) custom-call(f32[32,1024]{1,0:T(8,128)S(1)} %add.18.kept, f32[32,1024]{1,0:T(8,128)S(1)} %collective-permute-done.1.crossed, f32[32,1024]{1,0:T(8,128)S(1)} %collective-permute-done.2.swapped, ...), custom_call_target="tpu_custom_call" | custom-call | flops 838860800 | bytes 4194304 | tf_op jit(solution)/shard_map/middle/pallas_call | solution.py:323
  14.7 0.4 %collective-permute-start.3 = (f32[32,1024]{1,0:T(8,128)S(1)}, f32[32,1024]{1,0:T(8,128)S(1)}, u32[]{:S(2)}, u32[]{:S(2)}) collective-permute-start(f32[32,1024]{1,0:T(8,128)S(1)} %get-tuple-element.79), channel_id=1, source_target_pairs={{0,16},{16,0},{1,17},{17,1},{2,18},{18,2},{3,19},{19,3},{4,20},{20... | collective-permute-start | bytes 393224 | tf_op jit(solution)/shard_map/ppermute | solution.py:354
  15.1 0.0 copy-done
  15.1 0.4 %keep.4 = f32[32,1024]{1,0:T(8,128)S(1)} custom-call(f32[3,32,1024]{2,1,0:T(8,128)S(1)} %copy-done, bf16[64,256]{1,0:T(8,128)(2,1)S(1)} %get-tuple-element.70.row_hi, bf16[64,256]{1,0:T(8,128)(2,1)S(1)} %get-tuple-element.71.row_lo, bf16[256,1024]{1,0:T(8,128)(2,1)S(1)} %get-tuple-element.77.w_hi, bf16[256,1024]{1,0:T(8,128)(2,1)S(1)} %get-tuple-element.78.w_lo), custom_call_target="tpu_custom_call" | custom-call | flops 41943040 | bytes 4194304 | tf_op jit(solution)/shard_map/keep/pallas_call | solution.py:323
  15.4 0.6 %collective-permute-done.3 = f32[32,1024]{1,0:T(8,128)S(1)} collective-permute-done((f32[32,1024]{1,0:T(8,128)S(1)}, f32[32,1024]{1,0:T(8,128)S(1)}, u32[]{:S(2)}, u32[]{:S(2)}) %collective-permute-start.3) | collective-permute-done | bytes 131104 | tf_op jit(solution)/shard_map/ppermute | solution.py:354
  16.1 1.3 %collective-permute-start.4 = (f32[32,1024]{1,0:T(8,128)S(1)}, f32[32,1024]{1,0:T(8,128)S(1)}, u32[]{:S(2)}, u32[]{:S(2)}) collective-permute-start(f32[32,1024]{1,0:T(8,128)S(1)} %add.20.kept), channel_id=1, source_target_pairs={{0,16},{1,0},{2,3},{3,2},{4,5},{5,4},{6,7},{7,6},{8,9},{9,8},{10,1... | collective-permute-start | bytes 393224 | tf_op jit(solution)/shard_map/ppermute | solution.py:355
  17.3 0.8 %prepare.3 = (bf16[4,256,256]{2,1,0:T(8,128)(2,1)S(1)}, bf16[4,256,256]{2,1,0:T(8,128)(2,1)S(1)}, bf16[64,256]{1,0:T(8,128)(2,1)S(1)}, bf16[64,256]{1,0:T(8,128)...) custom-call(f32[4,16,128]{2,1,0:T(8,128)S(1)} %get-tuple-element.61.taps), custom_call_target="tpu_custom_call" | custom-call | flops 419430400 | bytes 4194304 | tf_op jit(solution)/shard_map/prepare/pallas_call | solution.py:323
  18.1 4.1 %collective-permute-done.4.crossed = f32[32,1024]{1,0:T(8,128)S(1)} collective-permute-done((f32[32,1024]{1,0:T(8,128)S(1)}, f32[32,1024]{1,0:T(8,128)S(1)}, u32[]{:S(2)}, u32[]{:S(2)}) %collective-permute-start.4) | collective-permute-done | bytes 131104 | tf_op jit(solution)/shard_map/ppermute | solution.py:355
  22.3 0.7 %collective-permute-start.5 = (f32[32,1024]{1,0:T(8,128)S(1)}, f32[32,1024]{1,0:T(8,128)S(1)}, u32[]{:S(2)}, u32[]{:S(2)}) collective-permute-start(f32[32,1024]{1,0:T(8,128)S(1)} %select_add_fusion.1), channel_id=1, source_target_pairs={{0,16},{16,0},{1,17},{17,1},{2,18},{18,2},{3,19},{19,3},{4,20},{20... | collective-permute-start | bytes 393224 | tf_op jit(solution)/shard_map/ppermute | solution.py:362
  23.0 1.0 %collective-permute-done.5.swapped = f32[32,1024]{1,0:T(8,128)S(1)} collective-permute-done((f32[32,1024]{1,0:T(8,128)S(1)}, f32[32,1024]{1,0:T(8,128)S(1)}, u32[]{:S(2)}, u32[]{:S(2)}) %collective-permute-start.5) | collective-permute-done | bytes 131104 | tf_op jit(solution)/shard_map/ppermute | solution.py:362
  23.9 1.7 %middle.3 = (f32[32,1024]{1,0:T(8,128)S(1)}, f32[4,32,1024]{2,1,0:T(8,128)S(1)}, bf16[256,1024]{1,0:T(8,128)(2,1)S(1)}, bf16[256,1024]{1,0:T(8,128)(2,1)S(1)}) custom-call(f32[32,1024]{1,0:T(8,128)S(1)} %add.20.kept, f32[32,1024]{1,0:T(8,128)S(1)} %collective-permute-done.4.crossed, f32[32,1024]{1,0:T(8,128)S(1)} %collective-permute-done.5.swapped, ...), custom_call_target="tpu_custom_call" | custom-call | flops 838860800 | bytes 4194304 | tf_op jit(solution)/shard_map/middle/pallas_call | solution.py:323
  25.7 0.4 %collective-permute-start.6 = (f32[32,1024]{1,0:T(8,128)S(1)}, f32[32,1024]{1,0:T(8,128)S(1)}, u32[]{:S(2)}, u32[]{:S(2)}) collective-permute-start(f32[32,1024]{1,0:T(8,128)S(1)} %get-tuple-element.98), channel_id=1, source_target_pairs={{0,16},{16,0},{1,17},{17,1},{2,18},{18,2},{3,19},{19,3},{4,20},{20... | collective-permute-start | bytes 393224 | tf_op jit(solution)/shard_map/ppermute | solution.py:354
  26.1 0.4 keep.5
  26.4 0.6 %collective-permute-done.6 = f32[32,1024]{1,0:T(8,128)S(1)} collective-permute-done((f32[32,1024]{1,0:T(8,128)S(1)}, f32[32,1024]{1,0:T(8,128)S(1)}, u32[]{:S(2)}, u32[]{:S(2)}) %collective-permute-start.6) | collective-permute-done | bytes 131104 | tf_op jit(solution)/shard_map/ppermute | solution.py:354
  27.1 1.1 %collective-permute-start.7 = (f32[32,1024]{1,0:T(8,128)S(1)}, f32[32,1024]{1,0:T(8,128)S(1)}, u32[]{:S(2)}, u32[]{:S(2)}) collective-permute-start(f32[32,1024]{1,0:T(8,128)S(1)} %add.22.kept), channel_id=1, source_target_pairs={{0,16},{1,0},{2,3},{3,2},{4,5},{5,4},{6,7},{7,6},{8,9},{9,8},{10,1... | collective-permute-start | bytes 393224 | tf_op jit(solution)/shard_map/ppermute | solution.py:355
  28.2 5.0 %collective-permute-done.7.crossed = f32[32,1024]{1,0:T(8,128)S(1)} collective-permute-done((f32[32,1024]{1,0:T(8,128)S(1)}, f32[32,1024]{1,0:T(8,128)S(1)}, u32[]{:S(2)}, u32[]{:S(2)}) %collective-permute-start.7) | collective-permute-done | bytes 131104 | tf_op jit(solution)/shard_map/ppermute | solution.py:355
  33.3 0.7 %collective-permute-start.8 = (f32[32,1024]{1,0:T(8,128)S(1)}, f32[32,1024]{1,0:T(8,128)S(1)}, u32[]{:S(2)}, u32[]{:S(2)}) collective-permute-start(f32[32,1024]{1,0:T(8,128)S(1)} %select_add_fusion), channel_id=1, source_target_pairs={{0,16},{16,0},{1,17},{17,1},{2,18},{18,2},{3,19},{19,3},{4,20},{20... | collective-permute-start | bytes 393224 | tf_op jit(solution)/shard_map/ppermute | solution.py:362
  34.0 1.0 %collective-permute-done.8.swapped = f32[32,1024]{1,0:T(8,128)S(1)} collective-permute-done((f32[32,1024]{1,0:T(8,128)S(1)}, f32[32,1024]{1,0:T(8,128)S(1)}, u32[]{:S(2)}, u32[]{:S(2)}) %collective-permute-start.8) | collective-permute-done | bytes 131104 | tf_op jit(solution)/shard_map/ppermute | solution.py:362
  34.9 1.6 %last.1 = (f32[4,32,1024]{2,1,0:T(8,128)}, f32[32,1024]{1,0:T(8,128)}) custom-call(f32[32,1024]{1,0:T(8,128)S(1)} %add.22.kept, f32[32,1024]{1,0:T(8,128)S(1)} %collective-permute-done.7.crossed, f32[32,1024]{1,0:T(8,128)S(1)} %collective-permute-done.8.swapped, bf16[4,2,256,256]{3,2,1,0:T(8,128)(2,1)S(1)} %get-tuple-element.101.adj, ...), custom_call_target="tpu_custom_call" | custom-call | flops 419430400 | bytes 4194304 | tf_op jit(solution)/shard_map/last/pallas_call | solution.py:323
  (6 shorter events, 0.1 us)
Async XLA Ops:
  3.3 1.7 %collective-permute-start = (f32[32,1024]{1,0:T(8,128)S(1)}, f32[32,1024]{1,0:T(8,128)S(1)}, u32[]{:S(2)}, u32[]{:S(2)}) collective-permute-start(f32[32,1024]{1,0:T(8,128)S(1)} %get-tuple-element.58), channel_id=1, source_target_pairs={{0,16},{16,0},{1,17},{17,1},{2,18},{18,2},{3,19},{19,3},{4,20},{20... | collective-permute-start | bytes 393224 | tf_op jit(solution)/shard_map/ppermute | solution.py:354
  5.1 5.3 %collective-permute-start.1 = (f32[32,1024]{1,0:T(8,128)S(1)}, f32[32,1024]{1,0:T(8,128)S(1)}, u32[]{:S(2)}, u32[]{:S(2)}) collective-permute-start(f32[32,1024]{1,0:T(8,128)S(1)} %add.18.kept), channel_id=1, source_target_pairs={{0,16},{1,0},{2,3},{3,2},{4,5},{5,4},{6,7},{7,6},{8,9},{9,8},{10,1... | collective-permute-start | bytes 393224 | tf_op jit(solution)/shard_map/ppermute | solution.py:355
  6.3 6.6 %copy-start.1 = (f32[4,32,1024]{2,1,0:T(8,128)S(1)}, f32[4,32,1024]{2,1,0:T(8,128)}, u32[]{:S(2)}) copy-start(f32[4,32,1024]{2,1,0:T(8,128)} %volume.3) | copy-start | bytes 1572868
  10.4 4.7 %copy-start = (f32[3,32,1024]{2,1,0:T(8,128)S(1)}, f32[3,32,1024]{2,1,0:T(8,128)}, u32[]{:S(2)}) copy-start(f32[3,32,1024]{2,1,0:T(8,128)} %measured.5) | copy-start | bytes 1179652
  10.4 2.5 %collective-permute-start.2 = (f32[32,1024]{1,0:T(8,128)S(1)}, f32[32,1024]{1,0:T(8,128)S(1)}, u32[]{:S(2)}, u32[]{:S(2)}) collective-permute-start(f32[32,1024]{1,0:T(8,128)S(1)} %select_add_fusion.2), channel_id=1, source_target_pairs={{0,16},{16,0},{1,17},{17,1},{2,18},{18,2},{3,19},{19,3},{4,20},{20... | collective-permute-start | bytes 393224 | tf_op jit(solution)/shard_map/ppermute | solution.py:362
  14.7 1.4 %collective-permute-start.3 = (f32[32,1024]{1,0:T(8,128)S(1)}, f32[32,1024]{1,0:T(8,128)S(1)}, u32[]{:S(2)}, u32[]{:S(2)}) collective-permute-start(f32[32,1024]{1,0:T(8,128)S(1)} %get-tuple-element.79), channel_id=1, source_target_pairs={{0,16},{16,0},{1,17},{17,1},{2,18},{18,2},{3,19},{19,3},{4,20},{20... | collective-permute-start | bytes 393224 | tf_op jit(solution)/shard_map/ppermute | solution.py:354
  16.1 6.2 %collective-permute-start.4 = (f32[32,1024]{1,0:T(8,128)S(1)}, f32[32,1024]{1,0:T(8,128)S(1)}, u32[]{:S(2)}, u32[]{:S(2)}) collective-permute-start(f32[32,1024]{1,0:T(8,128)S(1)} %add.20.kept), channel_id=1, source_target_pairs={{0,16},{1,0},{2,3},{3,2},{4,5},{5,4},{6,7},{7,6},{8,9},{9,8},{10,1... | collective-permute-start | bytes 393224 | tf_op jit(solution)/shard_map/ppermute | solution.py:355
  22.3 1.7 %collective-permute-start.5 = (f32[32,1024]{1,0:T(8,128)S(1)}, f32[32,1024]{1,0:T(8,128)S(1)}, u32[]{:S(2)}, u32[]{:S(2)}) collective-permute-start(f32[32,1024]{1,0:T(8,128)S(1)} %select_add_fusion.1), channel_id=1, source_target_pairs={{0,16},{16,0},{1,17},{17,1},{2,18},{18,2},{3,19},{19,3},{4,20},{20... | collective-permute-start | bytes 393224 | tf_op jit(solution)/shard_map/ppermute | solution.py:362
  25.7 1.4 %collective-permute-start.6 = (f32[32,1024]{1,0:T(8,128)S(1)}, f32[32,1024]{1,0:T(8,128)S(1)}, u32[]{:S(2)}, u32[]{:S(2)}) collective-permute-start(f32[32,1024]{1,0:T(8,128)S(1)} %get-tuple-element.98), channel_id=1, source_target_pairs={{0,16},{16,0},{1,17},{17,1},{2,18},{18,2},{3,19},{19,3},{4,20},{20... | collective-permute-start | bytes 393224 | tf_op jit(solution)/shard_map/ppermute | solution.py:354
  27.1 6.2 %collective-permute-start.7 = (f32[32,1024]{1,0:T(8,128)S(1)}, f32[32,1024]{1,0:T(8,128)S(1)}, u32[]{:S(2)}, u32[]{:S(2)}) collective-permute-start(f32[32,1024]{1,0:T(8,128)S(1)} %add.22.kept), channel_id=1, source_target_pairs={{0,16},{1,0},{2,3},{3,2},{4,5},{5,4},{6,7},{7,6},{8,9},{9,8},{10,1... | collective-permute-start | bytes 393224 | tf_op jit(solution)/shard_map/ppermute | solution.py:355
  33.3 1.7 %collective-permute-start.8 = (f32[32,1024]{1,0:T(8,128)S(1)}, f32[32,1024]{1,0:T(8,128)S(1)}, u32[]{:S(2)}, u32[]{:S(2)}) collective-permute-start(f32[32,1024]{1,0:T(8,128)S(1)} %select_add_fusion), channel_id=1, source_target_pairs={{0,16},{16,0},{1,17},{17,1},{2,18},{18,2},{3,19},{19,3},{4,20},{20... | collective-permute-start | bytes 393224 | tf_op jit(solution)/shard_map/ppermute | solution.py:362
